TPU v7x, 128 devices: a whole 4x4x4 slice. The times are simulated.
128 devices in a mesh: views: 32 (over x, y, core), heads: 4 (over z).
Axes of the slice: x: 4, y: 4, z: 4, core: 2. Of those that a mesh axis runs over, the one named last changes fastest.
Arguments:
- latents: bfloat16 [128, 256, 1024], P('views'), may hold values from -6 to 6
- norm_gain: float32 [1024], replicated, may hold values from 0.25 to 1.75
- w_qkv: bfloat16 [3, 1024, 1024], P(None, None, 'heads'), may hold values from -0.1875 to 0.1875
- w_out: bfloat16 [1024, 1024], P('heads'), may hold values from -0.1875 to 0.1875
- intersection: int32 [128, 2], replicated, may hold values 0 or 1
- match_block: int32 [32768, 1], P('views'), may hold values from 0 to 31; in each aligned block of 1024 rows (0 to 1023, 1024 to 2047, ...) at most 64 rows name the same one
- match_row: int32 [32768], P('views'), may hold values from 0 to 1023
- confidence: float32 [32768], P('views'), may hold values from 0.2 to 1
Outputs:
- refined: float32 [128, 256, 1024], P('views', None, 'heads')
Inputs may be any that keep to these rules, and one draw needn't show every extreme that they name: `match_block`: among the rows of one device (1024 aligned rows), at most 64 name the same block, and some block is named by exactly 64 of them.
All inputs are finite; a program needn't handle non-finite values.
Results may differ from a plain program's by a relative error of at most 0.012.
The roundings to bfloat16 on the way count: a program that leaves them out, or rounds other values in their place, can miss the bound.
Values may be sent and summed in bfloat16 or wider, within the bound.
A program may use at most 128 MiB of HBM per device.

v0:
```python
import jax
import jax.numpy as jnp
from jax import lax
from jax.sharding import PartitionSpec as P

D = 1024
HEADS = 16


neg_large = -1e30
coupling = 0.5
epsilon = 1e-06


def passed_along(x, axis, by):
    peers = lax.axis_size(axis)
    return lax.ppermute(x, axis, [(i, (i + by) % peers) for i in range(peers)])


def partial_block(queries, keys, values, head_dim):
    tokens = queries.shape[0]
    heads_here = queries.shape[1] // head_dim
    query_heads = queries.reshape(tokens, heads_here, head_dim)
    key_heads = keys.reshape(tokens, heads_here, head_dim)
    value_heads = values.reshape(tokens, heads_here, head_dim)
    scores = jnp.einsum(
        "qhd,khd->hqk", query_heads, key_heads, preferred_element_type=jnp.float32
    ) * head_dim ** (-0.5)
    maximum = jnp.max(scores, axis=-1)
    weights = jnp.exp(scores - maximum[..., None])
    totals = jnp.sum(weights, axis=-1)
    numerator = jnp.einsum(
        "hqk,khd->hqd",
        weights.astype(jnp.bfloat16),
        value_heads,
        preferred_element_type=jnp.float32,
    )
    return (maximum, totals, numerator)


def merge_into(running, piece_part, present):
    maximum, totals, numerator = running
    other_max, other_tot, other_num = piece_part
    other_max = jnp.where(present > 0, other_max, neg_large)
    highest = jnp.maximum(maximum, other_max)
    old_scale = jnp.exp(maximum - highest)
    new_scale = jnp.exp(other_max - highest) * present
    return (
        highest,
        totals * old_scale + other_tot * new_scale,
        numerator * old_scale[..., None] + other_num * new_scale[..., None],
    )


def per_device(latents, norm_gain, w_qkv, w_out, intersection, match_block, match_row, confidence):
    local_views, tokens, feature_width = latents.shape
    window = intersection.shape[1]
    sub_width = w_qkv.shape[2]
    head_dim = D // HEADS
    device_count = lax.axis_size("views")
    views_total = local_views * device_count
    first_view = lax.axis_index("views") * local_views
    head_group = lax.axis_index("heads")
    local_rows = local_views * tokens
    wide_latents = latents.astype(jnp.float32)
    mean_square = jnp.mean(wide_latents * wide_latents, axis=-1, keepdims=True)
    normed = (
        (wide_latents * lax.rsqrt(mean_square + epsilon) * norm_gain)
        .astype(jnp.bfloat16)
        .reshape(local_rows, feature_width)
    )
    joined_weight = jnp.concatenate([w_qkv[0], w_qkv[1], w_qkv[2]], axis=1)
    projected = jnp.dot(normed, joined_weight, preferred_element_type=jnp.float32).astype(
        jnp.bfloat16
    )
    projected = projected.reshape(local_views, tokens, 3 * sub_width)

    def split_parts(block):
        return (
            block[:, :sub_width],
            block[:, sub_width : 2 * sub_width],
            block[:, 2 * sub_width :],
        )

    running = []
    for source in range(local_views):
        queries, keys, values = split_parts(projected[source])
        running.append(partial_block(queries, keys, values, head_dim))
    ahead = passed_along(projected[:window], "views", -1)
    extended = jnp.concatenate([projected, ahead], axis=0)
    empty_max = jnp.full((sub_width // head_dim, tokens), neg_large, jnp.float32)
    empty_tot = jnp.zeros((sub_width // head_dim, tokens), jnp.float32)
    empty_num = jnp.zeros((sub_width // head_dim, tokens, head_dim), jnp.float32)
    outgoing = [(empty_max, empty_tot, empty_num) for slot_number in range(window)]
    for source in range(local_views):
        src_queries, src_keys, src_values = split_parts(projected[source])
        for offset in range(window):
            partner = source + offset + 1
            present = intersection[(first_view + source) % views_total, offset].astype(jnp.float32)
            par_queries, par_keys, par_values = split_parts(extended[partner])
            running[source] = merge_into(
                running[source], partial_block(src_queries, par_keys, par_values, head_dim), present
            )
            reverse_part = partial_block(par_queries, src_keys, src_values, head_dim)
            if partner < local_views:
                running[partner] = merge_into(running[partner], reverse_part, present)
            else:
                outgoing[partner - local_views] = merge_into(
                    outgoing[partner - local_views], reverse_part, present
                )
    sent_max = jnp.stack([entry[0] for entry in outgoing])
    sent_tot = jnp.stack([entry[1] for entry in outgoing])
    sent_num = jnp.stack([entry[2] for entry in outgoing])
    got_max, got_tot, got_num = passed_along((sent_max, sent_tot, sent_num), "views", 1)
    for slot_number in range(window):
        running[slot_number] = merge_into(
            running[slot_number],
            (got_max[slot_number], got_tot[slot_number], got_num[slot_number]),
            jnp.float32(1.0),
        )
    attended_views = []
    for source in range(local_views):
        maximum, totals, numerator = running[source]
        result = numerator / totals[..., None]
        attended_views.append(
            jnp.transpose(result, (1, 0, 2)).reshape(tokens, sub_width).astype(jnp.bfloat16)
        )
    attended = jnp.concatenate(attended_views, axis=0)
    group_terms = jnp.dot(attended, w_out, preferred_element_type=jnp.float32)
    summed = lax.psum_scatter(
        group_terms.astype(jnp.bfloat16), "heads", scatter_dimension=1, tiled=True
    ).astype(jnp.float32)
    own_features = lax.dynamic_slice_in_dim(
        latents.reshape(local_rows, feature_width), head_group * sub_width, sub_width, 1
    )
    layer_out = (own_features.astype(jnp.float32) + summed).astype(jnp.bfloat16)
    target_block = match_block[:, 0]
    capacity = 2 * local_rows // device_count
    onehot = (target_block[:, None] == jnp.arange(device_count, dtype=jnp.int32)[None, :]).astype(
        jnp.int32
    )
    earlier = jnp.cumsum(onehot, axis=0) - onehot
    slot_index = jnp.sum(earlier * onehot, axis=1)
    requests = (
        jnp.zeros((device_count, capacity), jnp.int32).at[target_block, slot_index].set(match_row)
    )
    row_values = layer_out[
        lax.all_to_all(requests, "views", split_axis=0, concat_axis=0, tiled=True)
    ]
    replies = lax.all_to_all(row_values, "views", split_axis=0, concat_axis=0, tiled=True)
    fetched = replies[target_block, slot_index]
    layer_wide = layer_out.astype(jnp.float32)
    refined = layer_wide + coupling * confidence[:, None] * (
        fetched.astype(jnp.float32) - layer_wide
    )
    return refined.reshape(local_views, tokens, sub_width)


def solution(mesh):
    in_specs = (
        P("views", None, None),
        P(),
        P(None, None, "heads"),
        P("heads", None),
        P(),
        P("views", None),
        P("views"),
        P("views"),
    )
    out_specs = P("views", None, "heads")
    return jax.shard_map(
        per_device, mesh=mesh, in_specs=in_specs, out_specs=out_specs, check_vma=False
    )
```

profile of v0, /device:TPU:1, one launch (start us, length us, event | category | flops | bytes accessed | tf_op | source)
XLA Modules:
  0.0 155.5 jit_solution(4672102943576815010)
XLA Ops:
  6.5 2.2 %fusion = f32[4,256]{1,0:T(4,128)S(1)} fusion(bf16[4,256,1024]{2,1,0:T(8,128)(2,1)} %param.8), kind=kLoop, calls=%fused_computation.5 | loop fusion | flops 3144704 | bytes 2101248 | tf_op jit(solution)/shard_map/reduce_sum | solution.py:66
  8.9 1.4 copy-done.1
  10.4 0.5 fusion.2
  10.9 1.8 %convolution_convert_fusion.1 = bf16[1024,768]{0,1:T(8,128)(2,1)S(1)} fusion(bf16[1024,1024]{1,0:T(8,128)(2,1)S(1)} %bitcast.547, bf16[1024,256]{1,0:T(8,128)(2,1)S(1)} %get-tuple-element.52, bf16[1024,256]{1,0:T(8,128)(2,1)S(1)} %get-tuple-element.53, bf16[1024,256]{1,0:T(8,128)(2,1)S(1)} %get-tuple-element.51), kind=kOutput, calls=%fused_computation.9 | convolution fusion | flops 1616117760 | bytes 5242880 | tf_op jit(solution)/shard_map/dot_general | solution.py:73
  12.8 1.1 copy-done.35
  14.0 1.2 copy.78
  15.1 1.4 collective-permute-start
  16.5 2.3 %fusion.243 = (bf16[256,256]{0,1:T(8,128)(2,1)S(1)}, bf16[256,256]{0,1:T(8,128)(2,1)S(1)}, bf16[256,256]{0,1:T(8,128)(2,1)S(1)}, bf16[256,256]{0,1:T(8,128)(2,1)...) fusion(bf16[1024,768]{0,1:T(8,128)(2,1)} %copy-done.35), kind=kLoop, calls=%fused_computation.377 | loop fusion | bytes 3145728 | tf_op jit(solution)/shard_map/slice | solution.py:80
  18.8 0.4 fusion.246
  19.2 0.4 fusion.250
  19.6 0.4 fusion.254
  19.9 0.4 fusion.253
  20.3 0.4 fusion.249
  20.7 0.4 fusion.255
  21.1 0.4 fusion.260
  21.5 0.4 fusion.259
  21.8 0.4 fusion.262
  22.2 0.4 fusion.251
  22.6 0.4 fusion.261
  23.0 0.4 fusion.263
  23.4 0.9 fusion.87
  24.3 0.9 fusion.83
  25.2 0.9 fusion.77
  26.1 0.9 fusion.73
  27.0 0.9 fusion.69
  27.9 0.9 fusion.65
  28.8 0.8 fusion.57
  29.6 0.7 constant_dynamic-slice_fusion.3
  35.2 1.3 fusion.265
  36.6 1.4 fusion.264
  38.0 1.0 fusion.53
  39.0 1.2 slice_bitcast_fusion.4
  40.2 0.9 fusion.244
  41.1 1.0 copy.46
  42.1 1.9 %fusion.248 = (f32[4,256]{1,0:T(4,128)}, f32[4,256,256]{1,2,0:T(8,128)}) fusion(bf16[256,4,64]{0,2,1:T(8,128)(2,1)S(1)} %bitcast.507, bf16[256,4,64]{0,2,1:T(8,128)(2,1)S(1)} %bitcast.551), kind=kOutput, calls=%fused_computation.382 | convolution fusion | flops 34077696 | bytes 1314816 | tf_op jit(solution)/shard_map/qhd,khd->hqk/dot_general | solution.py:26
  44.0 1.9 %fusion.252 = (f32[4,256]{1,0:T(4,128)}, f32[4,256,256]{1,2,0:T(8,128)}) fusion(bf16[256,4,64]{0,2,1:T(8,128)(2,1)S(1)} %bitcast.518, bf16[256,4,64]{0,2,1:T(8,128)(2,1)S(1)} %bitcast.552), kind=kOutput, calls=%fused_computation.386 | convolution fusion | flops 34077696 | bytes 1314816 | tf_op jit(solution)/shard_map/qhd,khd->hqk/dot_general | solution.py:26
  45.9 1.0 copy.33
  46.9 1.3 fusion.257
  48.3 1.4 fusion.258
  49.6 1.0 copy.53
  50.6 1.9 %fusion.247 = (f32[4,256]{1,0:T(4,128)}, f32[4,256,256]{1,2,0:T(8,128)}) fusion(bf16[256,4,64]{0,2,1:T(8,128)(2,1)S(1)} %bitcast.508, bf16[256,4,64]{0,2,1:T(8,128)(2,1)S(1)} %bitcast.556), kind=kOutput, calls=%fused_computation.381 | convolution fusion | flops 34077696 | bytes 1314816 | tf_op jit(solution)/shard_map/qhd,khd->hqk/dot_general | solution.py:26
  52.6 1.0 copy.47
  53.6 0.8 copy.54
  54.5 0.4 fusion.256
  55.0 0.7 copy-done.27
  57.2 1.4 collective-permute-start.2
  58.7 0.6 collective-permute-start.3
  59.2 1.2 collective-permute-start.1
  63.6 0.4 copy-done.11
  67.4 0.5 copy-done.25
  68.9 0.7 copy-done.32
  69.9 2.1 %convolution_convert_fusion = bf16[1024,1024]{1,0:T(8,128)(2,1)} fusion(bf16[256,1024]{1,0:T(8,128)(2,1)S(1)} %copy-done, bf16[256,256]{0,1:T(8,128)(2,1)S(1)} %bitcast.568, bf16[256,256]{0,1:T(8,128)(2,1)S(1)} %bitcast.567, bf16[256,256]{0,1:T(8,128)(2,1)S(1)} %bitcast.569, bf16[256,256]{0,1:T(8,128)(2,1)S(1)} %bitcast.570), kind=kOutput, calls=%fused_computation.8 | convolution fusion | flops 540016640 | bytes 3145728 | tf_op jit(solution)/shard_map/dot_general | solution.py:129
  72.0 9.0 %reduce-window.6 = s32[32,8,128]{2,1,0:T(8,128)S(1)} reduce-window(s32[32,8,128]{2,1,0:T(8,128)S(1)} %fusion.155, s32[]{:T(128)} %constant.64.clone.1), window={size=1x1x128 pad=0_0x0_0x127_0}, to_apply=%region_42.43 | reduce-window | flops 4161536 | bytes 262148 | tf_op jit(solution)/shard_map/reduce-window
  81.8 4.5 %scatter_custom_fusion = s32[2048]{0:T(1024)S(1)} fusion(s32[1024]{0:T(1024)S(1)} %broadcast_select_fusion, s32[1024]{0:T(1024)} %param.14, s32[]{:T(128)} %constant.64.clone.1), kind=kCustom, calls=%fused_computation.342 | custom fusion | bytes 8704
  86.3 0.7 all_to_all.11
  87.0 11.4 %all-to-all-start = ((s32[32,1,64]{2,1,0:T(1,128)}), s32[32,1,64]{2,1,0:T(1,128)S(1)}, u32[]{:S(2)}, u32[]{:S(2)}) async-start(s32[32,1,64]{2,1,0:T(1,128)} %all_to_all.11), calls=%async_computation.1 | async-start | bytes 32768 | tf_op jit(solution)/shard_map/all_to_all | solution.py:148
  98.4 7.0 %all-to-all-done = s32[32,1,64]{2,1,0:T(1,128)S(1)} async-done(((s32[32,1,64]{2,1,0:T(1,128)}), s32[32,1,64]{2,1,0:T(1,128)S(1)}, u32[]{:S(2)}, u32[]{:S(2)}) %all-to-all-start) | async-done | bytes 8224 | tf_op jit(solution)/shard_map/all_to_all | solution.py:148
  105.5 1.1 reduce-scatter.2.cloned.1.call-done
  106.5 1.2 add_convert_fusion
  107.7 9.1 %gather_fusion = bf16[2048,256]{1,0:T(8,128)(2,1)} fusion(bf16[1024,256]{1,0:T(8,128)(2,1)S(1)} %add_convert_fusion, s32[2048]{0:T(1024)S(1)} %broadcast_clamp_fusion), kind=kCustom, calls=%fused_computation | custom fusion | bytes 2105344 | tf_op jit(solution)/shard_map/gather | solution.py:147
  116.8 7.8 %all-to-all-start.1 = ((bf16[32,64,256]{2,1,0:T(8,128)(2,1)}), bf16[32,64,256]{2,1,0:T(8,128)(2,1)S(1)}, u32[]{:S(2)}, u32[]{:S(2)}) async-start(bf16[32,64,256]{2,1,0:T(8,128)(2,1)} %bitcast.90), calls=%async_computation.2 | async-start | bytes 2097152 | tf_op jit(solution)/shard_map/all_to_all | solution.py:150
  124.7 16.9 %all-to-all-done.1 = bf16[32,64,256]{2,1,0:T(8,128)(2,1)S(1)} async-done(((bf16[32,64,256]{2,1,0:T(8,128)(2,1)}), bf16[32,64,256]{2,1,0:T(8,128)(2,1)S(1)}, u32[]{:S(2)}, u32[]{:S(2)}) %all-to-all-start.1) | async-done | bytes 1048608 | tf_op jit(solution)/shard_map/all_to_all | solution.py:150
  141.6 5.8 %gather_fusion.1 = bf16[1024,256]{1,0:T(8,128)(2,1)S(1)} fusion(bf16[32,64,256]{2,1,0:T(8,128)(2,1)S(1)} %all-to-all-done.1, s32[1024]{0:T(1024)S(1)} %bitcast.497), kind=kCustom, calls=%fused_computation.1 | custom fusion | bytes 1056768 | tf_op jit(solution)/shard_map/gather | solution.py:151
  147.4 1.3 convert_add_fusion
  (239 shorter events, 10.3 us)
Async XLA Ops:
  6.5 63.3 %copy-start = (bf16[256,1024]{1,0:T(8,128)(2,1)S(1)}, bf16[256,1024]{1,0:T(8,128)(2,1)}, u32[]{:S(2)}) copy-start(bf16[256,1024]{1,0:T(8,128)(2,1)} %param.11) | copy-start | bytes 1572868
  6.5 100.0 %reduce-scatter.2.cloned.1.call-start = ((), (), s32[]{:S(2)}) async-start(), calls=%async_computation.3 | async-start | bytes 2621440 | tf_op jit(solution)/shard_map/reduce_scatter | solution.py:130
  6.5 2.3 %copy-start.40 = (bf16[3,1024,256]{2,1,0:T(8,128)(2,1)S(1)}, bf16[3,1024,256]{2,1,0:T(8,128)(2,1)}, u32[]{:S(2)}) copy-start(bf16[3,1024,256]{2,1,0:T(8,128)(2,1)} %param.10) | copy-start | bytes 4718596
  8.8 1.6 %copy-start.1 = (bf16[4,256,1024]{2,1,0:T(8,128)(2,1)S(1)}, bf16[4,256,1024]{2,1,0:T(8,128)(2,1)}, u32[]{:S(2)}) copy-start(bf16[4,256,1024]{2,1,0:T(8,128)(2,1)} %param.8) | copy-start | bytes 6291460
  8.8 1.6 %copy-start.88 = (f32[1024]{0:T(1024)S(1)}, f32[1024]{0:T(1024)}, u32[]{:S(2)}) copy-start(f32[1024]{0:T(1024)} %param.9) | copy-start | bytes 12292
  15.1 23.8 %collective-permute-start = (bf16[2,256,768]{2,1,0:T(8,128)(2,1)}, bf16[2,256,768]{2,1,0:T(8,128)(2,1)}, u32[]{:S(2)}, u32[]{:S(2)}) collective-permute-start(bf16[2,256,768]{2,1,0:T(8,128)(2,1)} %bitcast.555), channel_id=1, source_target_pairs={{0,124},{4,0},{8,4},{12,8},{16,12},{20,16},{24,20},{28,24},{32,28}... | collective-permute-start | bytes 2359304 | tf_op jit(solution)/shard_map/ppermute | solution.py:17
  18.8 3.8 %copy-start.38 = (bf16[256,256]{0,1:T(8,128)(2,1)}, bf16[256,256]{0,1:T(8,128)(2,1)S(1)}, u32[]{:S(2)}) copy-start(bf16[256,256]{0,1:T(8,128)(2,1)S(1)} %get-tuple-element.50) | copy-start | bytes 393220
  18.8 4.2 %copy-start.37 = (bf16[256,256]{0,1:T(8,128)(2,1)}, bf16[256,256]{0,1:T(8,128)(2,1)S(1)}, u32[]{:S(2)}) copy-start(bf16[256,256]{0,1:T(8,128)(2,1)S(1)} %get-tuple-element.39) | copy-start | bytes 393220
  19.2 5.1 %copy-start.20 = (f32[4,256,256]{1,2,0:T(8,128)}, f32[4,256,256]{1,2,0:T(8,128)S(1)}, u32[]{:S(2)}) copy-start(f32[4,256,256]{1,2,0:T(8,128)S(1)} %get-tuple-element.84) | copy-start | bytes 3145732
  19.2 5.1 %copy-start.58 = (f32[4,256]{1,0:T(4,128)}, f32[4,256]{1,0:T(4,128)S(1)}, u32[]{:S(2)}) copy-start(f32[4,256]{1,0:T(4,128)S(1)} %get-tuple-element.83) | copy-start | bytes 12292
  19.5 4.7 %copy-start.12 = (f32[4,256,256]{1,2,0:T(8,128)}, f32[4,256,256]{1,2,0:T(8,128)S(1)}, u32[]{:S(2)}) copy-start(f32[4,256,256]{1,2,0:T(8,128)S(1)} %get-tuple-element.92) | copy-start | bytes 3145732
  19.6 4.7 %copy-start.50 = (f32[4,256]{1,0:T(4,128)}, f32[4,256]{1,0:T(4,128)S(1)}, u32[]{:S(2)}) copy-start(f32[4,256]{1,0:T(4,128)S(1)} %get-tuple-element.91) | copy-start | bytes 12292
  19.9 5.2 %copy-start.10 = (f32[4,256,256]{1,2,0:T(8,128)}, f32[4,256,256]{1,2,0:T(8,128)S(1)}, u32[]{:S(2)}) copy-start(f32[4,256,256]{1,2,0:T(8,128)S(1)} %get-tuple-element.100) | copy-start | bytes 3145732
  19.9 5.2 %copy-start.48 = (f32[4,256]{1,0:T(4,128)}, f32[4,256]{1,0:T(4,128)S(1)}, u32[]{:S(2)}) copy-start(f32[4,256]{1,0:T(4,128)S(1)} %get-tuple-element.99) | copy-start | bytes 12292
  20.3 4.9 %copy-start.8 = (f32[4,256,256]{1,2,0:T(8,128)}, f32[4,256,256]{1,2,0:T(8,128)S(1)}, u32[]{:S(2)}) copy-start(f32[4,256,256]{1,2,0:T(8,128)S(1)} %get-tuple-element.98) | copy-start | bytes 3145732
  20.3 4.9 %copy-start.46 = (f32[4,256]{1,0:T(4,128)}, f32[4,256]{1,0:T(4,128)S(1)}, u32[]{:S(2)}) copy-start(f32[4,256]{1,0:T(4,128)S(1)} %get-tuple-element.97) | copy-start | bytes 12292
  20.7 2.7 %copy-start.16 = (f32[4,256,256]{1,2,0:T(8,128)}, f32[4,256,256]{1,2,0:T(8,128)S(1)}, u32[]{:S(2)}) copy-start(f32[4,256,256]{1,2,0:T(8,128)S(1)} %get-tuple-element.90) | copy-start | bytes 3145732
  20.7 2.7 %copy-start.54 = (f32[4,256]{1,0:T(4,128)}, f32[4,256]{1,0:T(4,128)S(1)}, u32[]{:S(2)}) copy-start(f32[4,256]{1,0:T(4,128)S(1)} %get-tuple-element.89) | copy-start | bytes 12292
  21.1 5.0 %copy-start.14 = (f32[4,256,256]{1,2,0:T(8,128)}, f32[4,256,256]{1,2,0:T(8,128)S(1)}, u32[]{:S(2)}) copy-start(f32[4,256,256]{1,2,0:T(8,128)S(1)} %get-tuple-element.102) | copy-start | bytes 3145732
  21.1 5.0 %copy-start.52 = (f32[4,256]{1,0:T(4,128)}, f32[4,256]{1,0:T(4,128)S(1)}, u32[]{:S(2)}) copy-start(f32[4,256]{1,0:T(4,128)S(1)} %get-tuple-element.101) | copy-start | bytes 12292
  21.4 5.6 %copy-start.2 = (f32[4,256,256]{1,2,0:T(8,128)}, f32[4,256,256]{1,2,0:T(8,128)S(1)}, u32[]{:S(2)}) copy-start(f32[4,256,256]{1,2,0:T(8,128)S(1)} %get-tuple-element.112) | copy-start | bytes 3145732
  21.8 5.2 %copy-start.29 = (f32[4,256,256]{1,2,0:T(8,128)}, f32[4,256,256]{1,2,0:T(8,128)S(1)}, u32[]{:S(2)}) copy-start(f32[4,256,256]{1,2,0:T(8,128)S(1)} %get-tuple-element.110) | copy-start | bytes 3145732
  21.8 5.2 %copy-start.65 = (f32[4,256]{1,0:T(4,128)}, f32[4,256]{1,0:T(4,128)S(1)}, u32[]{:S(2)}) copy-start(f32[4,256]{1,0:T(4,128)S(1)} %get-tuple-element.109) | copy-start | bytes 12292
  22.2 5.7 %copy-start.4 = (f32[4,256,256]{1,2,0:T(8,128)}, f32[4,256,256]{1,2,0:T(8,128)S(1)}, u32[]{:S(2)}) copy-start(f32[4,256,256]{1,2,0:T(8,128)S(1)} %get-tuple-element.116) | copy-start | bytes 3145732
  22.6 3.5 %copy-start.18 = (f32[4,256,256]{1,2,0:T(8,128)}, f32[4,256,256]{1,2,0:T(8,128)S(1)}, u32[]{:S(2)}) copy-start(f32[4,256,256]{1,2,0:T(8,128)S(1)} %get-tuple-element.94) | copy-start | bytes 3145732
  22.6 3.5 %copy-start.56 = (f32[4,256]{1,0:T(4,128)}, f32[4,256]{1,0:T(4,128)S(1)}, u32[]{:S(2)}) copy-start(f32[4,256]{1,0:T(4,128)S(1)} %get-tuple-element.93) | copy-start | bytes 12292
  23.0 5.0 %copy-start.6 = (f32[4,256,256]{1,2,0:T(8,128)}, f32[4,256,256]{1,2,0:T(8,128)S(1)}, u32[]{:S(2)}) copy-start(f32[4,256,256]{1,2,0:T(8,128)S(1)} %get-tuple-element.114) | copy-start | bytes 3145732
  23.0 4.9 %copy-start.44 = (f32[4,256]{1,0:T(4,128)}, f32[4,256]{1,0:T(4,128)S(1)}, u32[]{:S(2)}) copy-start(f32[4,256]{1,0:T(4,128)S(1)} %get-tuple-element.113) | copy-start | bytes 12292
  23.3 5.5 %copy-start.31 = (f32[4,256,256]{1,2,0:T(8,128)}, f32[4,256,256]{1,2,0:T(8,128)S(1)}, u32[]{:S(2)}) copy-start(f32[4,256,256]{1,2,0:T(8,128)S(1)} %get-tuple-element.118) | copy-start | bytes 3145732
  23.4 5.5 %copy-start.67 = (f32[4,256]{1,0:T(4,128)}, f32[4,256]{1,0:T(4,128)S(1)}, u32[]{:S(2)}) copy-start(f32[4,256]{1,0:T(4,128)S(1)} %get-tuple-element.117) | copy-start | bytes 12292
  27.9 1.7 %copy-start.86 = (s32[128,2]{0,1:T(2,128)S(1)}, s32[128,2]{0,1:T(2,128)}, u32[]{:S(2)}) copy-start(s32[128,2]{0,1:T(2,128)} %param.12) | copy-start | bytes 3076
  36.5 3.6 %copy-start.22 = (f32[4,256,256]{1,2,0:T(8,128)}, f32[4,256,256]{1,2,0:T(8,128)S(1)}, u32[]{:S(2)}) copy-start(f32[4,256,256]{1,2,0:T(8,128)S(1)} %get-tuple-element.122) | copy-start | bytes 3145732
  36.6 3.6 %copy-start.60 = (f32[4,256]{1,0:T(4,128)}, f32[4,256]{1,0:T(4,128)S(1)}, u32[]{:S(2)}) copy-start(f32[4,256]{1,0:T(4,128)S(1)} %get-tuple-element.121) | copy-start | bytes 12292
  38.0 3.1 %copy-start.24 = (f32[4,256,256]{1,2,0:T(8,128)}, f32[4,256,256]{1,2,0:T(8,128)S(1)}, u32[]{:S(2)}) copy-start(f32[4,256,256]{1,2,0:T(8,128)S(1)} %get-tuple-element.120) | copy-start | bytes 3145732
  38.0 3.0 %copy-start.62 = (f32[4,256]{1,0:T(4,128)}, f32[4,256]{1,0:T(4,128)S(1)}, u32[]{:S(2)}) copy-start(f32[4,256]{1,0:T(4,128)S(1)} %get-tuple-element.119) | copy-start | bytes 12292
  46.9 7.4 %copy-start.41 = (bf16[256,256]{1,0:T(8,128)(2,1)S(1)}, bf16[256,256]{1,0:T(8,128)(2,1)}, u32[]{:S(2)}) copy-start(bf16[256,256]{1,0:T(8,128)(2,1)} %get-tuple-element.125) | copy-start | bytes 393220
  48.3 5.3 %copy-start.42 = (bf16[256,256]{1,0:T(8,128)(2,1)S(1)}, bf16[256,256]{1,0:T(8,128)(2,1)}, u32[]{:S(2)}) copy-start(bf16[256,256]{1,0:T(8,128)(2,1)} %get-tuple-element.124) | copy-start | bytes 393220
  54.4 1.5 copy-start.28
  56.5 4.0 %copy-start.34 = (f32[4,256,256]{1,2,0:T(8,128)S(1)}, f32[4,256,256]{1,2,0:T(8,128)}, u32[]{:S(2)}) copy-start(f32[4,256,256]{1,2,0:T(8,128)} %get-tuple-element.86) | copy-start | bytes 3145732
  56.5 4.0 %copy-start.70 = (f32[4,256]{1,0:T(4,128)S(1)}, f32[4,256]{1,0:T(4,128)}, u32[]{:S(2)}) copy-start(f32[4,256]{1,0:T(4,128)} %get-tuple-element.85) | copy-start | bytes 12292
  56.8 3.9 %copy-start.26 = (f32[4,256,256]{1,2,0:T(8,128)S(1)}, f32[4,256,256]{1,2,0:T(8,128)}, u32[]{:S(2)}) copy-start(f32[4,256,256]{1,2,0:T(8,128)} %get-tuple-element.88) | copy-start | bytes 3145732
  56.8 3.9 %copy-start.64 = (f32[4,256]{1,0:T(4,128)S(1)}, f32[4,256]{1,0:T(4,128)}, u32[]{:S(2)}) copy-start(f32[4,256]{1,0:T(4,128)} %get-tuple-element.87) | copy-start | bytes 12292
  56.8 4.1 %copy-start.51 = (f32[4,256]{1,0:T(4,128)S(1)}, f32[4,256]{1,0:T(4,128)}, u32[]{:S(2)}) copy-start(f32[4,256]{1,0:T(4,128)} %copy-done.50) | copy-start | bytes 12292
  56.8 4.1 %copy-start.55 = (f32[4,256]{1,0:T(4,128)S(1)}, f32[4,256]{1,0:T(4,128)}, u32[]{:S(2)}) copy-start(f32[4,256]{1,0:T(4,128)} %copy-done.54) | copy-start | bytes 12292
  56.8 4.1 %copy-start.59 = (f32[4,256]{1,0:T(4,128)S(1)}, f32[4,256]{1,0:T(4,128)}, u32[]{:S(2)}) copy-start(f32[4,256]{1,0:T(4,128)} %copy-done.58) | copy-start | bytes 12292
  56.8 4.1 %copy-start.81 = (f32[4,256]{1,0:T(4,128)S(1)}, f32[4,256]{1,0:T(4,128)}, u32[]{:S(2)}) copy-start(f32[4,256]{1,0:T(4,128)} %fusion.87) | copy-start | bytes 12292
  56.8 4.1 %copy-start.82 = (f32[4,256]{1,0:T(4,128)S(1)}, f32[4,256]{1,0:T(4,128)}, u32[]{:S(2)}) copy-start(f32[4,256]{1,0:T(4,128)} %get-tuple-element.126) | copy-start | bytes 12292
  56.8 4.1 %copy-start.83 = (f32[4,256]{1,0:T(4,128)S(1)}, f32[4,256]{1,0:T(4,128)}, u32[]{:S(2)}) copy-start(f32[4,256]{1,0:T(4,128)} %get-tuple-element.127) | copy-start | bytes 12292
  57.1 3.8 %copy-start.21 = (f32[4,256,256]{1,2,0:T(8,128)S(1)}, f32[4,256,256]{1,2,0:T(8,128)}, u32[]{:S(2)}) copy-start(f32[4,256,256]{1,2,0:T(8,128)} %copy-done.20) | copy-start | bytes 3145732
  57.2 3.8 %copy-start.36 = (bf16[256,256]{0,1:T(8,128)(2,1)S(1)}, bf16[256,256]{0,1:T(8,128)(2,1)}, u32[]{:S(2)}) copy-start(bf16[256,256]{0,1:T(8,128)(2,1)} %get-tuple-element.47) | copy-start | bytes 393220
  57.2 4.1 %copy-start.33 = (f32[4,256,256]{1,2,0:T(8,128)S(1)}, f32[4,256,256]{1,2,0:T(8,128)}, u32[]{:S(2)}) copy-start(f32[4,256,256]{1,2,0:T(8,128)} %get-tuple-element.96) | copy-start | bytes 3145732
  57.2 4.1 %copy-start.69 = (f32[4,256]{1,0:T(4,128)S(1)}, f32[4,256]{1,0:T(4,128)}, u32[]{:S(2)}) copy-start(f32[4,256]{1,0:T(4,128)} %get-tuple-element.95) | copy-start | bytes 12292
  57.2 11.3 %collective-permute-start.2 = (f32[2,4,256,64]{2,3,1,0:T(8,128)S(1)}, f32[2,4,256,64]{2,3,1,0:T(8,128)S(1)}, u32[]{:S(2)}, u32[]{:S(2)}) collective-permute-start(f32[2,4,256,64]{2,3,1,0:T(8,128)S(1)} %pad_maximum_fusion), channel_id=1, source_target_pairs={{0,4},{4,8},{8,12},{12,16},{16,20},{20,24},{24,28},{28,32},{32,36}... | collective-permute-start | bytes 1572872 | tf_op jit(solution)/shard_map/ppermute | solution.py:17
  58.7 7.2 %collective-permute-start.3 = (f32[2,4,256]{2,1,0:T(4,128)S(1)}, f32[2,4,256]{2,1,0:T(4,128)S(1)}, u32[]{:S(2)}, u32[]{:S(2)}) collective-permute-start(f32[2,4,256]{2,1,0:T(4,128)S(1)} %pad_maximum_fusion.2), channel_id=1, source_target_pairs={{0,4},{4,8},{8,12},{12,16},{16,20},{20,24},{24,28},{28,32},{32,36}... | collective-permute-start | bytes 24584 | tf_op jit(solution)/shard_map/ppermute | solution.py:17
  59.2 6.7 %collective-permute-start.1 = (f32[2,4,256]{2,1,0:T(4,128)S(1)}, f32[2,4,256]{2,1,0:T(4,128)S(1)}, u32[]{:S(2)}, u32[]{:S(2)}) collective-permute-start(f32[2,4,256]{2,1,0:T(4,128)S(1)} %pad_maximum_fusion.1), channel_id=1, source_target_pairs={{0,4},{4,8},{8,12},{12,16},{16,20},{20,24},{24,28},{28,32},{32,36}... | collective-permute-start | bytes 24584 | tf_op jit(solution)/shard_map/ppermute | solution.py:17
  65.1 1.6 %copy-start.5 = (f32[4,256,256]{1,2,0:T(8,128)S(1)}, f32[4,256,256]{1,2,0:T(8,128)}, u32[]{:S(2)}) copy-start(f32[4,256,256]{1,2,0:T(8,128)} %copy-done.4) | copy-start | bytes 3145732
  66.6 1.6 %copy-start.23 = (f32[4,256,256]{1,2,0:T(8,128)S(1)}, f32[4,256,256]{1,2,0:T(8,128)}, u32[]{:S(2)}) copy-start(f32[4,256,256]{1,2,0:T(8,128)} %copy-done.22) | copy-start | bytes 3145732
  67.0 1.5 copy-start.30
  69.9 2.1 %copy-start.71 = (s32[1024,1]{0,1:T(1,128)S(1)}, s32[1024,1]{0,1:T(1,128)}, u32[]{:S(2)}) copy-start(s32[1024,1]{0,1:T(1,128)} %param.13) | copy-start | bytes 12292
  72.0 9.6 %copy-start.90 = (s32[2]{0:T(128)S(1)}, s32[2]{0:T(128)}, u32[]{:S(2)}) copy-start(s32[2]{0:T(128)} %constant.86) | copy-start | bytes 28
  72.0 9.7 %copy-start.89 = (s32[2]{0:T(128)S(1)}, s32[2]{0:T(128)}, u32[]{:S(2)}) copy-start(s32[2]{0:T(128)} %constant.89) | copy-start | bytes 28
  87.0 18.4 %all-to-all-start = ((s32[32,1,64]{2,1,0:T(1,128)}), s32[32,1,64]{2,1,0:T(1,128)S(1)}, u32[]{:S(2)}, u32[]{:S(2)}) async-start(s32[32,1,64]{2,1,0:T(1,128)} %all_to_all.11), calls=%async_computation.1 | async-start | bytes 32768 | tf_op jit(solution)/shard_map/all_to_all | solution.py:148
  116.8 7.9 %copy-start.87 = (f32[1024]{0:T(1024)S(1)}, f32[1024]{0:T(1024)}, u32[]{:S(2)}) copy-start(f32[1024]{0:T(1024)} %param.15) | copy-start | bytes 12292
  116.8 24.8 %all-to-all-start.1 = ((bf16[32,64,256]{2,1,0:T(8,128)(2,1)}), bf16[32,64,256]{2,1,0:T(8,128)(2,1)S(1)}, u32[]{:S(2)}, u32[]{:S(2)}) async-start(bf16[32,64,256]{2,1,0:T(8,128)(2,1)} %bitcast.90), calls=%async_computation.2 | async-start | bytes 2097152 | tf_op jit(solution)/shard_map/all_to_all | solution.py:150
  (34 other events, 37.1 us)
Sparse Core Ops, SparseCore 0:
  72.1 34.3 reduce-scatter.1
where the time goes:
time: 156 us; the launch traced here: 155 us
  local copies, waits for them, and re-layouts  38.4 us (25%)
  matrix products  25.7 us (16%)
  waiting for transfers between devices  25 us (16%)
  starting transfers between devices  23.8 us (15%)
  other arithmetic  23 us (15%)
  between operations  19.7 us (13%)
    all_to_all x1, waiting for transfers between devices, per_device(): lax.all_to_all(row_values, 'views', split_axis=0, concat_axis=0, tiled=True)  16.9 us
    dot_general x20, matrix products, partial_block(): jnp.einsum('qhd,khd->hqk', query_heads, key_heads, preferred_element_type...  15.8 us
    all_to_all x1, starting transfers between devices, per_device(): lax.all_to_all(requests, 'views', split_axis=0, concat_axis=0, tiled=True)  11.4 us
    unnamed x183, local copies, waits for them, and re-layouts  11.3 us
    another operation x3, other arithmetic  9.15 us
    gather x1, local copies, waits for them, and re-layouts, per_device(): layer_out[lax.all_to_all(requests, 'views', split_axis=0, concat_axis=0,...  9.06 us
    reduce_sum x14, other arithmetic, partial_block(): totals = jnp.sum(weights, axis=-1)  8.04 us
    all_to_all x1, starting transfers between devices, per_device(): lax.all_to_all(row_values, 'views', split_axis=0, concat_axis=0, tiled=True)  7.85 us
  transfers between devices with their start and end apart: 7, of which 3 were waited for; matrix products, arithmetic and copies ran while one was open for 23% of the time, Pallas kernels for 0%

commit v1 on v0

v1 whole, which is shorter than its diff:
```python
import functools

import jax
import jax.numpy as jnp
from jax import lax
from jax.experimental import pallas as pl
from jax.experimental.pallas import tpu as pltpu
from jax.sharding import PartitionSpec as P

MESH = pl.DeviceIdType.MESH
F32, BF16, I32 = jnp.float32, jnp.bfloat16, jnp.int32
EPSILON = 1e-06
COUPLING = 0.5
HEAD_DIM = 64
ORDER = (1, 2, 0, 3)


def dot(a, b):
    return jnp.dot(a, b, preferred_element_type=F32)


def dot_nt(a, b):
    return lax.dot_general(a, b, (((1,), (1,)), ((), ())), preferred_element_type=F32)


def kernel(
    nv, views_total, cap,
    lat, gain, wqkv, wout, inter, mb, mr, conf,
    out,
    kv, q, att, wo, lay, gsel, fsel, idxs, reqo, reqi, rows, reps,
    kv_s, kv_r, wo_s, wo_r, at_s, at_r, fw_s, fw_r, rq_s, rq_r, rp_s, rp_r,
):
    nl, tok, width = lat.shape
    sub = wqkv.shape[2]
    half = tok // 2
    me = lax.axis_index("views")
    z = lax.axis_index("heads")
    up, down, far = lax.rem(z + 1, 4), lax.rem(z + 3, 4), lax.rem(z + 2, 4)
    nxt, prv = lax.rem(me + 1, nv), lax.rem(me + nv - 1, nv)

    def remote(src, dst, send, recv, device):
        return pltpu.make_async_remote_copy(
            src_ref=src, dst_ref=dst, send_sem=send, recv_sem=recv,
            device_id=device, device_id_type=MESH,
        )

    barrier = pltpu.get_barrier_semaphore()

    def greet(k, carry):
        pl.semaphore_signal(
            barrier, inc=1, device_id=(lax.rem(me + k, nv), z), device_id_type=MESH
        )
        return carry

    lax.fori_loop(1, nv, greet, 0)
    for other in (up, down, far):
        pl.semaphore_signal(barrier, inc=1, device_id=(me, other), device_id_type=MESH)

    def kv_copy(i):
        slot, target = ((nl + 2 + i, prv) if i < 2 else (i - 2, nxt))
        return remote(kv.at[2 + i], kv.at[slot], kv_s.at[i], kv_r.at[i], (target, z))

    def wo_copy(rel):
        target = (z, up, far, down)[rel]
        cols = pl.ds(pl.multiple_of(target * sub, sub), sub)
        return remote(wout.at[:, cols], wo.at[rel], wo_s.at[rel], wo_r.at[rel], (me, target))

    def att_copy(i, way):
        return remote(
            att.at[i, 0], att.at[i, (1, 3)[way]], at_s.at[i, way], at_r.at[i, way],
            (me, (up, down)[way]),
        )

    def fwd_copy(i, way):
        part = pl.ds(way * half, half)
        return remote(
            att.at[i, (1, 3)[way], part], att.at[i, 2, part], fw_s.at[i, way], fw_r.at[i, way],
            (me, (up, down)[way]),
        )

    def req_copy(k):
        return remote(reqo.at[k], reqi.at[k], rq_s.at[k], rq_r.at[k], (lax.rem(me + k, nv), z))

    def rep_copy(k):
        return remote(
            rows.at[k], reps.at[k], rp_s.at[k], rp_r.at[k], (lax.rem(me + nv - k, nv), z)
        )

    for n, i in enumerate((3, 0, 1, 2)):
        wide = lat[i].astype(F32)
        mean_square = jnp.mean(wide * wide, axis=-1, keepdims=True)
        x = (wide * lax.rsqrt(mean_square + EPSILON) * gain[...]).astype(BF16)
        kv[2 + i, :, :sub] = dot(x, wqkv[1]).astype(BF16)
        kv[2 + i, :, sub:] = dot(x, wqkv[2]).astype(BF16)
        q[i] = (dot(x, wqkv[0]).astype(BF16).astype(F32) * HEAD_DIM ** (-0.5)).astype(BF16)
        if n == 0:
            pl.semaphore_wait(barrier, nv + 2)
            for rel in (1, 2, 3):
                wo_copy(rel).start()
        kv_copy(i).start()

    rel_block = mb[...] - me
    rel_block = jnp.where(rel_block < 0, rel_block + nv, rel_block)
    wanted = mr[...]
    lanes = mb.shape[1]
    block_iota = lax.broadcasted_iota(I32, (nv, lanes), 0)
    slot_iota = lax.broadcasted_iota(I32, (lanes, lanes), 0)
    before = (slot_iota < lax.broadcasted_iota(I32, (lanes, lanes), 1)).astype(F32).astype(BF16)
    base = jnp.zeros((nv, 1), F32)
    digits = jnp.zeros((2 * nv, lanes), F32)
    for c in range(mb.shape[0]):
        onehot = (rel_block[c : c + 1] == block_iota).astype(F32)
        earlier = dot(onehot.astype(BF16), before) + base
        slot = jnp.sum(onehot * earlier, axis=0, keepdims=True)
        base = base + jnp.sum(onehot, axis=1, keepdims=True)
        idxs[c : c + 1, :] = rel_block[c : c + 1].astype(F32) * cap + slot
        is_slot = (slot.astype(I32) == slot_iota).astype(F32).astype(BF16)
        row = wanted[c : c + 1]
        high, low = (row >> 5).astype(F32), (row & 31).astype(F32)
        both = jnp.concatenate([onehot * high, onehot * low], axis=0).astype(BF16)
        digits = digits + dot_nt(both, is_slot)
    requests = (digits[:nv] * 32.0 + digits[nv:]).astype(I32)
    for k in range(nv):
        reqo[k] = jnp.broadcast_to(requests[k : k + 1], reqo.shape[1:])
    reqi[0] = jnp.broadcast_to(requests[0:1], reqo.shape[1:])

    def send_request(k, carry):
        req_copy(k).start()
        return carry

    lax.fori_loop(1, nv, send_request, 0)

    lane = lax.broadcasted_iota(I32, (1, 2 * HEAD_DIM), 1)
    first = lane < HEAD_DIM

    def attend(i):
        a = me * nl + i
        bias = []
        for j in range(5):
            d = j - 2
            if d == 0:
                bias.append(None)
            else:
                source = a if d > 0 else lax.rem(a + d + views_total, views_total)
                present = inter[source * 2 + (abs(d) - 1)]
                bias.append((present.astype(F32) - 1.0) * 1e30)
        for t in range(sub // (2 * HEAD_DIM)):
            k_cols = slice(2 * HEAD_DIM * t, 2 * HEAD_DIM * (t + 1))
            v_cols = slice(sub + 2 * HEAD_DIM * t, sub + 2 * HEAD_DIM * (t + 1))
            pair = q[i, :, k_cols]
            done = []
            for mine in (first, jnp.logical_not(first)):
                query = jnp.where(mine, pair, jnp.zeros_like(pair))
                scores = []
                for j in range(5):
                    s = dot_nt(query, kv[i + j, :, k_cols])
                    scores.append(s if bias[j] is None else s + bias[j])
                top = functools.reduce(jnp.maximum, scores)
                top = jnp.max(top, axis=-1, keepdims=True)
                numer, total = None, None
                for j in range(5):
                    p = jnp.exp(scores[j] - top)
                    total = p if total is None else total + p
                    part = dot(p.astype(BF16), kv[i + j, :, v_cols])
                    numer = part if numer is None else numer + part
                total = jnp.sum(total, axis=-1, keepdims=True)
                done.append(numer / total)
            att[i, 0, :, k_cols] = jnp.where(first, done[0], done[1]).astype(BF16)

    def forward(i):
        for way in (0, 1):
            att_copy(i, way).wait_recv()
            fwd_copy(i, way).start()

    for n, i in enumerate(ORDER):
        if n == 0:
            kv_copy(3).wait_recv()
        elif n == 1:
            kv_copy(0).wait_recv()
        elif n == 2:
            kv_copy(2).wait_recv()
        else:
            kv_copy(1).wait_recv()
        attend(i)
        for way in (0, 1):
            att_copy(i, way).start()
        if n > 0:
            forward(ORDER[n - 1])

    n_slots = nv * cap
    places = jnp.transpose(idxs[...])
    for c in range(mb.shape[0]):
        place = places[:, c : c + 1].astype(I32)
        hit = place == lax.broadcasted_iota(I32, (lanes, n_slots), 1)
        fsel[lanes * c : lanes * (c + 1), :] = hit.astype(F32).astype(BF16)

    def take_request(k, carry):
        req_copy(k).wait()
        return carry

    lax.fori_loop(1, nv, take_request, 0)
    asked = jnp.transpose(reqi[:, 0, :])
    for k in range(nv):
        hit = asked[:cap, k : k + 1] == lax.broadcasted_iota(I32, (cap, nl * tok), 1)
        gsel[cap * k : cap * (k + 1), :] = hit.astype(F32).astype(BF16)

    forward(ORDER[-1])

    for rel in (1, 2, 3):
        wo_copy(rel).wait()

    own = pl.ds(pl.multiple_of(z * sub, sub), sub)
    for i in ORDER:
        for way in (0, 1):
            fwd_copy(i, way).wait_recv()
        proj = dot(att[i, 0], wout[:, own]).astype(BF16).astype(F32)
        for rel in (1, 2, 3):
            proj = proj + dot(att[i, rel], wo[rel]).astype(BF16).astype(F32)
        lay[tok * i : tok * (i + 1), :] = (lat[i, :, own].astype(F32) + proj).astype(BF16)

    group = 8
    for g in range(nv // group):
        picked = dot(gsel[group * cap * g : group * cap * (g + 1), :], lay[...]).astype(BF16)
        picked = picked.reshape(group, cap, sub)
        rows[group * g : group * (g + 1)] = picked
        if g == 0:
            reps[0] = picked[0]

        def send_reply(k, carry):
            rep_copy(k).start()
            return carry

        lax.fori_loop(max(1, group * g), group * (g + 1), send_reply, 0)

    for g in range(nv // group):

        def take_reply(k, carry):
            rep_copy(k).wait()
            return carry

        lax.fori_loop(max(1, group * g), group * (g + 1), take_reply, 0)
        block = reps[group * g : group * (g + 1)].reshape(group * cap, sub)
        part = dot(fsel[:, group * cap * g : group * cap * (g + 1)], block)
        if g == 0:
            out[...] = part
        else:
            out[...] += part

    weight = COUPLING * jnp.transpose(conf[...])
    for c in range(mb.shape[0]):
        here = slice(lanes * c, lanes * (c + 1))
        mine = lay[here, :].astype(F32)
        out[here, :] = mine + weight[:, c : c + 1] * (out[here, :] - mine)

    for i in range(nl):
        kv_copy(i).wait_send()
        for way in (0, 1):
            att_copy(i, way).wait_send()
            fwd_copy(i, way).wait_send()


def per_device(nv, latents, norm_gain, w_qkv, w_out, intersection, match_block, match_row, confidence):
    nl, tok, width = latents.shape
    sub = w_qkv.shape[2]
    rows = nl * tok
    cap = 2 * rows // nv
    vmem = pl.BlockSpec(memory_space=pltpu.VMEM)
    smem = pl.BlockSpec(memory_space=pltpu.SMEM)
    dma = pltpu.SemaphoreType.DMA
    lanes = 128
    result = pl.pallas_call(
        functools.partial(kernel, nv, nl * nv, cap),
        out_shape=jax.ShapeDtypeStruct((rows, sub), F32),
        in_specs=[vmem, vmem, vmem, vmem, smem, vmem, vmem, vmem],
        out_specs=vmem,
        scratch_shapes=[
            pltpu.VMEM((nl + 4, tok, 2 * sub), BF16),
            pltpu.VMEM((nl, tok, sub), BF16),
            pltpu.VMEM((nl, 4, tok, sub), BF16),
            pltpu.VMEM((4, sub, sub), BF16),
            pltpu.VMEM((rows, sub), BF16),
            pltpu.VMEM((nv * cap, rows), BF16),
            pltpu.VMEM((rows, nv * cap), BF16),
            pltpu.VMEM((rows // lanes, lanes), F32),
            pltpu.VMEM((nv, 8, lanes), I32),
            pltpu.VMEM((nv, 8, lanes), I32),
            pltpu.VMEM((nv, cap, sub), BF16),
            pltpu.VMEM((nv, cap, sub), BF16),
            dma((nl,)), dma((nl,)), dma((4,)), dma((4,)),
            dma((nl, 2)), dma((nl, 2)), dma((nl, 2)), dma((nl, 2)),
            dma((nv,)), dma((nv,)), dma((nv,)), dma((nv,)),
        ],
        compiler_params=pltpu.CompilerParams(
            collective_id=0, has_side_effects=True, vmem_limit_bytes=60 * 1024 * 1024
        ),
    )(
        latents,
        norm_gain.reshape(1, width),
        w_qkv,
        w_out,
        intersection.reshape(-1),
        match_block.reshape(rows // lanes, lanes),
        match_row.reshape(rows // lanes, lanes),
        confidence.reshape(rows // lanes, lanes),
    )
    return result.reshape(nl, tok, sub)


def solution(mesh):
    in_specs = (
        P("views", None, None),
        P(),
        P(None, None, "heads"),
        P("heads", None),
        P(),
        P("views", None),
        P("views"),
        P("views"),
    )
    out_specs = P("views", None, "heads")
    return jax.shard_map(
        functools.partial(per_device, mesh.shape["views"]),
        mesh=mesh, in_specs=in_specs, out_specs=out_specs, check_vma=False,
    )
```

time: 156 us -> 61.8 us (0.40)
  Pallas kernels: 0 us -> 57.2 us
  local copies, waits for them, and re-layouts: 38.4 us -> 3.77 us
  matrix products: 25.7 us -> 0 us
  waiting for transfers between devices: 25 us -> 0 us
  starting transfers between devices: 23.8 us -> 0 us
  other arithmetic: 23 us -> 0 us
  between operations: 19.7 us -> 0.01 us
    pallas_call x0 -> x1, Pallas kernels: none -> 57.2 us  [per_device(): pl.pallas_call(functools.partial(kernel, nv, nl * nv, cap), out_shape=jax...]
    dot_general x42 -> x0, matrix products: 25.7 us -> none  [the longest x20 15.8 us: partial_block(): jnp.einsum('qhd,khd->hqk', query_heads, key_heads, preferred_element_type...]
    all_to_all x2 -> x0, waiting for transfers between devices: 23.9 us -> none  [the longest x1 16.9 us: per_device(): lax.all_to_all(row_values, 'views', split_axis=0, concat_axis=0, tiled=True)]
    all_to_all x2 -> x0, starting transfers between devices: 19.3 us -> none  [the longest x1 11.4 us: per_device(): lax.all_to_all(requests, 'views', split_axis=0, concat_axis=0, tiled=True)]
    gather x2 -> x0, local copies, waits for them, and re-layouts: 14.9 us -> none  [the longest x1 9.06 us: per_device(): layer_out[lax.all_to_all(requests, 'views', split_axis=0, concat_axis=0,...]
    reduce_sum x16 -> x0, other arithmetic: 10.3 us -> none  [the longest x14 8.04 us: partial_block(): totals = jnp.sum(weights, axis=-1)]
    slice x12 -> x0, local copies, waits for them, and re-layouts: 9.45 us -> none  [the longest x4 4.25 us: split_parts(): block[:, :sub_width]]
    another operation x8 -> x0, other arithmetic: 9.22 us -> none
  transfers between devices with their start and end apart: 7 -> 0, of which waited for: 3 -> 0; matrix products, arithmetic and copies ran while one was open for 23% -> 0% of each run, Pallas kernels for 0% -> 0%
where the time goes in v1:
time: 61.8 us; the launch traced here: 60.9 us
  Pallas kernels  57.2 us (93%)
  local copies, waits for them, and re-layouts  3.77 us (6%)
    pallas_call x1, Pallas kernels, per_device(): pl.pallas_call(functools.partial(kernel, nv, nl * nv, cap), out_shape=jax...  57.2 us
    unnamed x2, local copies, waits for them, and re-layouts  3.07 us

profile of v1, /device:TPU:1, one launch (start us, length us, event | category | flops | bytes accessed | tf_op | source)
XLA Modules:
  0.0 60.9 jit_solution(2700095094495438796)
XLA Ops:
  0.0 0.8 %copy.9 = s32[128,2]{1,0:T(8,128)S(1)} copy(s32[128,2]{0,1:T(2,128)} %param.12) | data formatting | bytes 2048 | tf_op args[4]
  0.8 0.7 %reshape.19.inter = s32[256]{0:T(256)} reshape(s32[128,2]{1,0:T(8,128)S(1)} %copy.9) | data formatting | bytes 2048 | tf_op jit(solution)/shard_map/reshape | solution.py:301
  1.5 57.2 %shard_map.82 = f32[1024,256]{1,0:T(8,128)} custom-call(bf16[4,256,1024]{2,1,0:T(8,128)(2,1)} %lat.1, f32[1,1024]{1,0:T(1,128)} %bitcast.6, bf16[3,1024,256]{2,1,0:T(8,128)(2,1)} %wqkv.1, bf16[256,1024]{1,0:T(8,128)(2,1)} %wout.1, s32[256]{0:T(256)} %reshape.19.inter, s32[8,128]{1,0:T(8,128)} %bitcast.7, s32[8,128]{1,0:T(8,128)} %bitcast.8, f32[8,128]{1,0:T(8,128)} %bitcast.9), custom_call_target="tpu_custom_call" | custom-call | tf_op jit(solution)/shard_map/pallas_call | solution.py:271
  58.6 2.3 %copy.11 = f32[4,256,256]{2,1,0:T(8,128)} copy(f32[4,256,256]{2,1,0:T(8,128)} %bitcast.5) | data formatting | bytes 2097152

commit v2 on v1

v2 whole, which is shorter than its diff:
```python
import functools

import jax
import jax.numpy as jnp
from jax import lax
from jax.experimental import pallas as pl
from jax.experimental.pallas import tpu as pltpu
from jax.sharding import PartitionSpec as P

MESH = pl.DeviceIdType.MESH
F32, BF16, I32 = jnp.float32, jnp.bfloat16, jnp.int32
EPSILON = 1e-06
COUPLING = 0.5
HEAD_DIM = 64
ORDER = (1, 2, 0, 3)
SIDE = 4


def ring_steps(d):
    return min(d, SIDE - d)


PLACES = sorted(
    ((dx, dy, dc) for dx in range(SIDE) for dy in range(SIDE) for dc in range(2)),
    key=lambda p: (-ring_steps(p[0]) - ring_steps(p[1]), -p[2]),
)
PICK_GROUPS = ((0, 4), (4, 8), (8, 16), (16, 24), (24, 32))
TAKE_GROUPS = ((0, 8), (8, 16), (16, 24), (24, 32))


def dot(a, b):
    return jnp.dot(a, b, preferred_element_type=F32)


def dot_nt(a, b):
    return lax.dot_general(a, b, (((1,), (1,)), ((), ())), preferred_element_type=F32)


def scope(name):
    return jax.named_scope(name)


def kernel(
    nv, views_total, cap,
    lat_h, gain_h, wqkv_h, wout_h, inter_h, mb_h, mr_h,
    lay_out, got_out,
    lat, gain, wqkv, wout, inter, mb, mr,
    kv, q, att, wo, part_s, part_r, lay, gsel, fsel, idxs, reqo, reqi, rows, reps, acc, got,
    in_sem, out_sem, kv_s, kv_r, wo_s, wo_r, at_s, at_r, pt_s, pt_r, rq_s, rq_r, rp_s, rp_r,
):
    nl, tok, width = lat.shape
    sub = wqkv.shape[2]
    me = lax.axis_index("views")
    z = lax.axis_index("heads")
    odd = lax.rem(z, 2)
    pair, opp = z + 1 - 2 * odd, lax.rem(z + 3 + 2 * odd, 4)
    pair_opp = lax.rem(pair + 3 + 2 * (1 - odd), 4)
    nxt, prv = lax.rem(me + 1, nv), lax.rem(me + nv - 1, nv)
    px, py, pc = me // (2 * SIDE), lax.rem(me // 2, SIDE), lax.rem(me, 2)

    def away(o, sign):
        dx, dy, dc = PLACES[o]
        bx = lax.rem(px + (dx if sign > 0 else SIDE - dx), SIDE)
        by = lax.rem(py + (dy if sign > 0 else SIDE - dy), SIDE)
        return bx * (2 * SIDE) + by * 2 + lax.rem(pc + dc, 2)

    def load(n, src, dst):
        copy = pltpu.make_async_copy(src, dst, in_sem.at[n])
        copy.start()
        return copy

    in_gain = load(0, gain_h, gain)
    in_lat = {3: load(1, lat_h.at[3], lat.at[3])}
    in_k = load(2, wqkv_h.at[1], wqkv.at[1])
    in_v = load(3, wqkv_h.at[2], wqkv.at[2])
    in_q = load(4, wqkv_h.at[0], wqkv.at[0])
    in_wout = load(5, wout_h, wout)
    for i in (0, 1, 2):
        in_lat[i] = load(6 + i, lat_h.at[i], lat.at[i])
    in_small = [load(9, mb_h, mb), load(10, mr_h, mr), load(11, inter_h, inter)]

    def remote(src, dst, send, recv, device):
        return pltpu.make_async_remote_copy(
            src_ref=src, dst_ref=dst, send_sem=send, recv_sem=recv,
            device_id=device, device_id_type=MESH,
        )

    barrier = pltpu.get_barrier_semaphore()

    def greet(k, carry):
        pl.semaphore_signal(
            barrier, inc=1, device_id=(lax.rem(me + k, nv), z), device_id_type=MESH
        )
        return carry

    lax.fori_loop(1, nv, greet, 0)
    for other in (pair, opp):
        pl.semaphore_signal(barrier, inc=1, device_id=(me, other), device_id_type=MESH)

    def kv_copy(i):
        slot, target = ((nl + 2 + i, prv) if i < 2 else (i - 2, nxt))
        return remote(kv.at[2 + i], kv.at[slot], kv_s.at[i], kv_r.at[i], (target, z))

    def wo_copy(n):
        cols = pl.ds(pl.multiple_of((pair, pair_opp)[n] * sub, sub), sub)
        return remote(wout.at[:, cols], wo.at[n], wo_s.at[n], wo_r.at[n], (me, pair))

    def att_copy(i):
        return remote(att.at[i, 0], att.at[i, 1], at_s.at[i], at_r.at[i], (me, pair))

    def part_copy(i):
        return remote(part_s.at[i], part_r.at[i], pt_s.at[i], pt_r.at[i], (me, opp))

    def req_copy(o):
        return remote(reqo.at[o], reqi.at[o], rq_s.at[o], rq_r.at[o], (away(o, 1), z))

    def rep_copy(o):
        return remote(rows.at[o], reps.at[o], rp_s.at[o], rp_r.at[o], (away(o, -1), z))

    in_gain.wait()
    for n, i in enumerate((3, 0, 1, 2)):
        with scope(f"proj{n}"):
            in_lat[i].wait()
            wide = lat[i].astype(F32)
            mean_square = jnp.mean(wide * wide, axis=-1, keepdims=True)
            x = (wide * lax.rsqrt(mean_square + EPSILON) * gain[...]).astype(BF16)
            if n == 0:
                in_k.wait()
            kv[2 + i, :, :sub] = dot(x, wqkv[1]).astype(BF16)
            if n == 0:
                in_v.wait()
            kv[2 + i, :, sub:] = dot(x, wqkv[2]).astype(BF16)
            if n == 0:
                in_q.wait()
            q[i] = (dot(x, wqkv[0]).astype(BF16).astype(F32) * HEAD_DIM ** (-0.5)).astype(BF16)
        if n == 0:
            with scope("greeted"):
                pl.semaphore_wait(barrier, nv + 1)
        kv_copy(i).start()
        if n == 0:
            in_wout.wait()
            for k in (0, 1):
                wo_copy(k).start()

    with scope("prep"):
        for copy in in_small:
            copy.wait()
        named = mb[...]
        rel = (((named >> 3) - px) & 3) * 8 + ((((named >> 1) & 3) - py) & 3) * 2 + ((named - pc) & 1)
        place = jnp.zeros_like(rel)
        for o, (dx, dy, dc) in enumerate(PLACES):
            place = jnp.where(rel == dx * 8 + dy * 2 + dc, o, place)
        wanted = mr[...]
        lanes = mb.shape[1]
        block_iota = lax.broadcasted_iota(I32, (nv, lanes), 0)
        slot_iota = lax.broadcasted_iota(I32, (lanes, lanes), 0)
        before = (slot_iota < lax.broadcasted_iota(I32, (lanes, lanes), 1)).astype(F32).astype(BF16)
        base = jnp.zeros((nv, 1), F32)
        digits = jnp.zeros((2 * nv, lanes), F32)
        for c in range(mb.shape[0]):
            onehot = (place[c : c + 1] == block_iota).astype(F32)
            earlier = dot(onehot.astype(BF16), before) + base
            slot = jnp.sum(onehot * earlier, axis=0, keepdims=True)
            base = base + jnp.sum(onehot, axis=1, keepdims=True)
            idxs[c : c + 1, :] = place[c : c + 1].astype(F32) * cap + slot
            is_slot = (slot.astype(I32) == slot_iota).astype(F32).astype(BF16)
            row = wanted[c : c + 1]
            high, low = (row >> 5).astype(F32), (row & 31).astype(F32)
            both = jnp.concatenate([onehot * high, onehot * low], axis=0).astype(BF16)
            digits = digits + dot_nt(both, is_slot)
        requests = (digits[:nv] * 32.0 + digits[nv:]).astype(I32)
        for k in range(nv):
            reqo[k] = jnp.broadcast_to(requests[k : k + 1], reqo.shape[1:])
        reqi[nv - 1] = jnp.broadcast_to(requests[nv - 1 : nv], reqo.shape[1:])
        for o in range(nv - 1):
            req_copy(o).start()

    lane = lax.broadcasted_iota(I32, (1, 2 * HEAD_DIM), 1)
    first = lane < HEAD_DIM

    def attend(i):
        a = me * nl + i
        bias = []
        for j in range(5):
            d = j - 2
            if d == 0:
                bias.append(None)
            else:
                source = a if d > 0 else lax.rem(a + d + views_total, views_total)
                present = inter[abs(d) - 1, source]
                bias.append((present.astype(F32) - 1.0) * 1e30)
        for t in range(sub // (2 * HEAD_DIM)):
            k_cols = slice(2 * HEAD_DIM * t, 2 * HEAD_DIM * (t + 1))
            v_cols = slice(sub + 2 * HEAD_DIM * t, sub + 2 * HEAD_DIM * (t + 1))
            both = q[i, :, k_cols]
            done = []
            for mine in (first, jnp.logical_not(first)):
                query = jnp.where(mine, both, jnp.zeros_like(both))
                scores = []
                for j in range(5):
                    s = dot_nt(query, kv[i + j, :, k_cols])
                    scores.append(s if bias[j] is None else s + bias[j])
                top = functools.reduce(jnp.maximum, scores)
                top = jnp.max(top, axis=-1, keepdims=True)
                numer, total = None, None
                for j in range(5):
                    p = jnp.exp(scores[j] - top)
                    total = p if total is None else total + p
                    part = dot(p.astype(BF16), kv[i + j, :, v_cols])
                    numer = part if numer is None else numer + part
                total = jnp.sum(total, axis=-1, keepdims=True)
                done.append(numer / total)
            att[i, 0, :, k_cols] = jnp.where(first, done[0], done[1]).astype(BF16)

    own = pl.ds(pl.multiple_of(z * sub, sub), sub)
    theirs = pl.ds(pl.multiple_of(opp * sub, sub), sub)

    def rounded(a, b):
        return dot(a, b).astype(BF16).astype(F32)

    def pass_on(i):
        att_copy(i).wait_recv()
        summed = rounded(att[i, 0], wout[:, theirs]) + rounded(att[i, 1], wo[1])
        part_s[i] = summed.astype(BF16)
        part_copy(i).start()

    def finish(i):
        proj = rounded(att[i, 0], wout[:, own]) + rounded(att[i, 1], wo[0])
        part_copy(i).wait_recv()
        proj = proj + part_r[i].astype(F32)
        lay[tok * i : tok * (i + 1), :] = (lat[i, :, own].astype(F32) + proj).astype(BF16)

    n_slots = nv * cap

    def select_mine():
        places = jnp.transpose(idxs[...])
        for c in range(mb.shape[0]):
            at = places[:, c : c + 1].astype(I32)
            hit = at == lax.broadcasted_iota(I32, (lanes, n_slots), 1)
            fsel[lanes * c : lanes * (c + 1), :] = hit.astype(F32).astype(BF16)

    def select_asked():
        for o in range(nv - 1):
            req_copy(o).wait()
        asked = jnp.transpose(reqi[:, 0, :])
        for k in range(nv):
            hit = asked[:cap, k : k + 1] == lax.broadcasted_iota(I32, (cap, nl * tok), 1)
            gsel[cap * k : cap * (k + 1), :] = hit.astype(F32).astype(BF16)

    for n, i in enumerate(ORDER):
        with scope(f"halo{n}"):
            kv_copy((3, 0, 2, 1)[n]).wait_recv()
        with scope(f"att{n}"):
            attend(i)
        att_copy(i).start()
        if n == 1:
            for k in (0, 1):
                wo_copy(k).wait()
        if n > 1:
            with scope(f"pass{n}"):
                pass_on(ORDER[n - 2])

    with scope("sel_mine"):
        select_mine()
    with scope("pass4"):
        pass_on(ORDER[2])
    with scope("sel_asked"):
        select_asked()
    with scope("pass5"):
        pass_on(ORDER[3])
    for n, i in enumerate(ORDER):
        with scope(f"finish{n}"):
            finish(i)
    lay_copy = pltpu.make_async_copy(lay, lay_out, out_sem.at[0])
    lay_copy.start()

    for lo, hi in PICK_GROUPS:
        with scope(f"pick{lo}"):
            picked = dot(gsel[cap * lo : cap * hi, :], lay[...]).astype(BF16)
            picked = picked.reshape(hi - lo, cap, sub)
            rows[lo:hi] = picked
            if hi == nv:
                reps[nv - 1] = picked[-1]
            for o in range(lo, min(hi, nv - 1)):
                rep_copy(o).start()

    for lo, hi in TAKE_GROUPS:
        with scope(f"take{lo}"):
            for o in range(lo, min(hi, nv - 1)):
                rep_copy(o).wait()
            block = reps[lo:hi].reshape((hi - lo) * cap, sub)
            part = dot(fsel[:, cap * lo : cap * hi], block)
            if lo > 0:
                part = acc[...] + part
            if hi < nv:
                acc[...] = part
            else:
                got[...] = part.astype(BF16)
    got_copy = pltpu.make_async_copy(got, got_out, out_sem.at[1])
    got_copy.start()

    for i in range(nl):
        kv_copy(i).wait_send()
        att_copy(i).wait_send()
        part_copy(i).wait_send()
    lay_copy.wait()
    got_copy.wait()


def per_device(nv, latents, norm_gain, w_qkv, w_out, intersection, match_block, match_row, confidence):
    nl, tok, width = latents.shape
    sub = w_qkv.shape[2]
    rows = nl * tok
    cap = 2 * rows // nv
    here = pl.BlockSpec(memory_space=pl.ANY)
    dma = pltpu.SemaphoreType.DMA
    vmem = pltpu.VMEM
    lanes = 128
    lay, got = pl.pallas_call(
        functools.partial(kernel, nv, nl * nv, cap),
        out_shape=[jax.ShapeDtypeStruct((rows, sub), BF16)] * 2,
        in_specs=[here] * 7,
        out_specs=[here] * 2,
        scratch_shapes=[
            vmem((nl, tok, width), BF16),
            vmem((1, width), F32),
            vmem((3, width, sub), BF16),
            vmem((sub, width), BF16),
            pltpu.SMEM(intersection.shape[::-1], I32),
            vmem((rows // lanes, lanes), I32),
            vmem((rows // lanes, lanes), I32),
            vmem((nl + 4, tok, 2 * sub), BF16),
            vmem((nl, tok, sub), BF16),
            vmem((nl, 2, tok, sub), BF16),
            vmem((2, sub, sub), BF16),
            vmem((nl, tok, sub), BF16),
            vmem((nl, tok, sub), BF16),
            vmem((rows, sub), BF16),
            vmem((nv * cap, rows), BF16),
            vmem((rows, nv * cap), BF16),
            vmem((rows // lanes, lanes), F32),
            vmem((nv, 8, lanes), I32),
            vmem((nv, 8, lanes), I32),
            vmem((nv, cap, sub), BF16),
            vmem((nv, cap, sub), BF16),
            vmem((rows, sub), F32),
            vmem((rows, sub), BF16),
            dma((12,)), dma((2,)),
            dma((nl,)), dma((nl,)), dma((2,)), dma((2,)),
            dma((nl,)), dma((nl,)), dma((nl,)), dma((nl,)),
            dma((nv,)), dma((nv,)), dma((nv,)), dma((nv,)),
        ],
        compiler_params=pltpu.CompilerParams(
            collective_id=0, has_side_effects=True, vmem_limit_bytes=60 * 1024 * 1024
        ),
    )(
        latents,
        norm_gain.reshape(1, width),
        w_qkv,
        w_out,
        intersection.T,
        match_block.reshape(rows // lanes, lanes),
        match_row.reshape(rows // lanes, lanes),
    )
    mine = lay.astype(F32)
    refined = mine + COUPLING * confidence[:, None] * (got.astype(F32) - mine)
    return refined.reshape(nl, tok, sub)


def solution(mesh):
    in_specs = (
        P("views", None, None),
        P(),
        P(None, None, "heads"),
        P("heads", None),
        P(),
        P("views", None),
        P("views"),
        P("views"),
    )
    out_specs = P("views", None, "heads")
    return jax.shard_map(
        functools.partial(per_device, mesh.shape["views"]),
        mesh=mesh, in_specs=in_specs, out_specs=out_specs, check_vma=False,
    )
```

time: 61.8 us -> 56 us (0.906); the launches traced: 60.9 us -> 55.9 us
  Pallas kernels: 57.2 us -> 52.7 us
  local copies, waits for them, and re-layouts: 3.77 us -> 0 us
  other arithmetic: 0 us -> 3.17 us
    pallas_call x1, Pallas kernels: 57.2 us -> 52.7 us  [per_device(): pl.pallas_call(functools.partial(kernel, nv, nl * nv, cap), out_shape=[ja...]
    unnamed x2 -> x0, local copies, waits for them, and re-layouts: 3.07 us -> none
    add x0 -> x1, other arithmetic: none -> 2.48 us  [per_device(): refined = mine + COUPLING * confidence[:, None] * (got.astype(F32) - mine)]
    reshape x1 -> x0, local copies, waits for them, and re-layouts: 0.7 us -> none  [per_device(): intersection.reshape(-1)]
    mul x0 -> x1, other arithmetic: none -> 0.69 us  [per_device(): refined = mine + COUPLING * confidence[:, None] * (got.astype(F32) - mine)]
where the time goes in v2:
time: 56 us; the launch traced here: 55.9 us
  Pallas kernels  52.7 us (94%)
  other arithmetic  3.17 us (6%)
    pallas_call x1, Pallas kernels, per_device(): pl.pallas_call(functools.partial(kernel, nv, nl * nv, cap), out_shape=[ja...  52.7 us
    add x1, other arithmetic, per_device(): refined = mine + COUPLING * confidence[:, None] * (got.astype(F32) - mine)  2.48 us

profile of v2, /device:TPU:1, one launch (start us, length us, event | category | flops | bytes accessed | tf_op | source)
XLA Modules:
  0.0 55.9 jit_solution(14604027619043305075)
XLA Ops:
  0.0 0.7 %broadcast_multiply_fusion = f32[1024]{0:T(1024)S(1)} fusion(f32[1024]{0:T(1024)} %param.15), kind=kLoop, calls=%fused_computation.3 | loop fusion | flops 1024 | bytes 8192 | tf_op jit(solution)/shard_map/mul | solution.py:366
  0.7 52.7 %shard_map.82 = (bf16[1024,256]{1,0:T(8,128)(2,1)}, bf16[1024,256]{1,0:T(8,128)(2,1)}) custom-call(bf16[4,256,1024]{2,1,0:T(8,128)(2,1)} %lat_h.1, f32[1,1024]{1,0:T(1,128)} %bitcast.5, bf16[3,1024,256]{2,1,0:T(8,128)(2,1)} %wqkv_h.1, bf16[256,1024]{1,0:T(8,128)(2,1)} %wout_h.1, s32[2,128]{1,0:T(2,128)} %bitcast.8, s32[8,128]{1,0:T(8,128)} %bitcast.6, ...), custom_call_target="tpu_custom_call" | custom-call | tf_op jit(solution)/shard_map/pallas_call | solution.py:319
  53.4 2.5 %convert_add_fusion = f32[1024,256]{1,0:T(8,128)} fusion(bf16[1024,256]{1,0:T(8,128)(2,1)} %get-tuple-element.7, bf16[1024,256]{1,0:T(8,128)(2,1)} %get-tuple-element.8, f32[1024]{0:T(1024)S(1)} %broadcast_multiply_fusion), kind=kLoop, calls=%fused_computation | loop fusion | flops 1310720 | bytes 2101248 | tf_op jit(solution)/shard_map/add | solution.py:366

commit v3 on v2

--- a/solution.py
+++ b/solution.py
@@ -12,8 +12,9 @@
 EPSILON = 1e-06
 COUPLING = 0.5
 HEAD_DIM = 64
-ORDER = (1, 2, 0, 3)
+ORDER = (1, 0, 2, 3)
 SIDE = 4
+VMEM_MIB = 60
 
 
 def ring_steps(d):
@@ -45,8 +46,8 @@
     lat_h, gain_h, wqkv_h, wout_h, inter_h, mb_h, mr_h,
     lay_out, got_out,
     lat, gain, wqkv, wout, inter, mb, mr,
-    kv, q, att, wo, part_s, part_r, lay, gsel, fsel, idxs, reqo, reqi, rows, reps, acc, got,
-    in_sem, out_sem, kv_s, kv_r, wo_s, wo_r, at_s, at_r, pt_s, pt_r, rq_s, rq_r, rp_s, rp_r,
+    kv, q, att, wo, part_s, part_r, lay, gsel, fsel, idxs, reqo, reqi, rows, reps, acc, normed,
+    in_sem, kv_s, kv_r, wo_s, wo_r, at_s, at_r, pt_s, pt_r, rq_s, rq_r, rp_s, rp_r,
 ):
     nl, tok, width = lat.shape
     sub = wqkv.shape[2]
@@ -54,9 +55,13 @@
     z = lax.axis_index("heads")
     odd = lax.rem(z, 2)
     pair, opp = z + 1 - 2 * odd, lax.rem(z + 3 + 2 * odd, 4)
-    pair_opp = lax.rem(pair + 3 + 2 * (1 - odd), 4)
-    nxt, prv = lax.rem(me + 1, nv), lax.rem(me + nv - 1, nv)
+    far = lax.rem(z + 2, 4)
     px, py, pc = me // (2 * SIDE), lax.rem(me // 2, SIDE), lax.rem(me, 2)
+    partner = me + 1 - 2 * pc
+    beyond = lax.rem(me + nv - 1 + 2 * pc, nv)
+
+    def actual(u):
+        return u * pc + (nl - 1 - u) * (1 - pc)
 
     def away(o, sign):
         dx, dy, dc = PLACES[o]
@@ -70,13 +75,13 @@
         return copy
 
     in_gain = load(0, gain_h, gain)
-    in_lat = {3: load(1, lat_h.at[3], lat.at[3])}
+    in_lat = {3: load(1, lat_h.at[actual(3)], lat.at[3])}
     in_k = load(2, wqkv_h.at[1], wqkv.at[1])
     in_v = load(3, wqkv_h.at[2], wqkv.at[2])
+    for u in (2, 0, 1):
+        in_lat[u] = load(6 + u, lat_h.at[actual(u)], lat.at[u])
+    in_wout = load(5, wout_h, wout)
     in_q = load(4, wqkv_h.at[0], wqkv.at[0])
-    in_wout = load(5, wout_h, wout)
-    for i in (0, 1, 2):
-        in_lat[i] = load(6 + i, lat_h.at[i], lat.at[i])
     in_small = [load(9, mb_h, mb), load(10, mr_h, mr), load(11, inter_h, inter)]
 
     def remote(src, dst, send, recv, device):
@@ -97,19 +102,24 @@
     for other in (pair, opp):
         pl.semaphore_signal(barrier, inc=1, device_id=(me, other), device_id_type=MESH)
 
-    def kv_copy(i):
-        slot, target = ((nl + 2 + i, prv) if i < 2 else (i - 2, nxt))
-        return remote(kv.at[2 + i], kv.at[slot], kv_s.at[i], kv_r.at[i], (target, z))
+    def kv_copy(u):
+        slot = (1, 0, nl + 3, nl + 2)[u]
+        target = partner if u < 2 else beyond
+        return remote(kv.at[2 + u], kv.at[slot], kv_s.at[u], kv_r.at[u], (target, z))
 
     def wo_copy(n):
-        cols = pl.ds(pl.multiple_of((pair, pair_opp)[n] * sub, sub), sub)
-        return remote(wout.at[:, cols], wo.at[n], wo_s.at[n], wo_r.at[n], (me, pair))
-
-    def att_copy(i):
-        return remote(att.at[i, 0], att.at[i, 1], at_s.at[i], at_r.at[i], (me, pair))
-
-    def part_copy(i):
-        return remote(part_s.at[i], part_r.at[i], pt_s.at[i], pt_r.at[i], (me, opp))
+        cols = pl.ds(pl.multiple_of((pair, far, opp, far)[n] * sub, sub), sub)
+        target = (pair, opp)[n // 2]
+        return remote(wout.at[:, cols], wo.at[n], wo_s.at[n], wo_r.at[n], (me, target))
+
+    def ways(n):
+        return (pair, opp) if n % 2 == 0 else (opp, pair)
+
+    def att_copy(n):
+        return remote(att.at[n, 0], att.at[n, 1], at_s.at[n], at_r.at[n], (me, ways(n)[0]))
+
+    def part_copy(n):
+        return remote(part_s.at[n], part_r.at[n], pt_s.at[n], pt_r.at[n], (me, ways(n)[1]))
 
     def req_copy(o):
         return remote(reqo.at[o], reqi.at[o], rq_s.at[o], rq_r.at[o], (away(o, 1), z))
@@ -118,40 +128,45 @@
         return remote(rows.at[o], reps.at[o], rp_s.at[o], rp_r.at[o], (away(o, -1), z))
 
     in_gain.wait()
-    for n, i in enumerate((3, 0, 1, 2)):
+    for n, u in enumerate((3, 2, 0, 1)):
         with scope(f"proj{n}"):
-            in_lat[i].wait()
-            wide = lat[i].astype(F32)
+            in_lat[u].wait()
+            wide = lat[u].astype(F32)
             mean_square = jnp.mean(wide * wide, axis=-1, keepdims=True)
             x = (wide * lax.rsqrt(mean_square + EPSILON) * gain[...]).astype(BF16)
+            normed[u] = x
             if n == 0:
                 in_k.wait()
-            kv[2 + i, :, :sub] = dot(x, wqkv[1]).astype(BF16)
+            kv[2 + u, :, :sub] = dot(x, wqkv[1]).astype(BF16)
             if n == 0:
                 in_v.wait()
-            kv[2 + i, :, sub:] = dot(x, wqkv[2]).astype(BF16)
-            if n == 0:
-                in_q.wait()
-            q[i] = (dot(x, wqkv[0]).astype(BF16).astype(F32) * HEAD_DIM ** (-0.5)).astype(BF16)
-        if n == 0:
+            kv[2 + u, :, sub:] = dot(x, wqkv[2]).astype(BF16)
+        if n == 2:
             with scope("greeted"):
                 pl.semaphore_wait(barrier, nv + 1)
-        kv_copy(i).start()
-        if n == 0:
+            for early in (0, 3, 2):
+                kv_copy(early).start()
             in_wout.wait()
-            for k in (0, 1):
+            for k in range(4):
                 wo_copy(k).start()
-
-    with scope("prep"):
-        for copy in in_small:
-            copy.wait()
+    kv_copy(1).start()
+    in_q.wait()
+    for copy in in_small:
+        copy.wait()
+
+    def ask(u):
+        found = dot(normed[u], wqkv[0]).astype(BF16).astype(F32)
+        q[u] = (found * HEAD_DIM ** (-0.5)).astype(BF16)
+
+    lanes = mb.shape[1]
+
+    def prepare():
         named = mb[...]
         rel = (((named >> 3) - px) & 3) * 8 + ((((named >> 1) & 3) - py) & 3) * 2 + ((named - pc) & 1)
         place = jnp.zeros_like(rel)
         for o, (dx, dy, dc) in enumerate(PLACES):
             place = jnp.where(rel == dx * 8 + dy * 2 + dc, o, place)
         wanted = mr[...]
-        lanes = mb.shape[1]
         block_iota = lax.broadcasted_iota(I32, (nv, lanes), 0)
         slot_iota = lax.broadcasted_iota(I32, (lanes, lanes), 0)
         before = (slot_iota < lax.broadcasted_iota(I32, (lanes, lanes), 1)).astype(F32).astype(BF16)
@@ -178,15 +193,16 @@
     lane = lax.broadcasted_iota(I32, (1, 2 * HEAD_DIM), 1)
     first = lane < HEAD_DIM
 
-    def attend(i):
-        a = me * nl + i
+    def attend(n, i):
+        a = me * nl + actual(i)
         bias = []
         for j in range(5):
             d = j - 2
             if d == 0:
                 bias.append(None)
             else:
-                source = a if d > 0 else lax.rem(a + d + views_total, views_total)
+                back = d * (1 - pc) if d > 0 else -d * pc
+                source = lax.rem(a - back + views_total, views_total)
                 present = inter[abs(d) - 1, source]
                 bias.append((present.astype(F32) - 1.0) * 1e30)
         for t in range(sub // (2 * HEAD_DIM)):
@@ -210,25 +226,29 @@
                     numer = part if numer is None else numer + part
                 total = jnp.sum(total, axis=-1, keepdims=True)
                 done.append(numer / total)
-            att[i, 0, :, k_cols] = jnp.where(first, done[0], done[1]).astype(BF16)
-
-    own = pl.ds(pl.multiple_of(z * sub, sub), sub)
-    theirs = pl.ds(pl.multiple_of(opp * sub, sub), sub)
+            att[n, 0, :, k_cols] = jnp.where(first, done[0], done[1]).astype(BF16)
+
+    own, to_pair, to_opp = (
+        pl.ds(pl.multiple_of(g * sub, sub), sub) for g in (z, pair, opp)
+    )
 
     def rounded(a, b):
         return dot(a, b).astype(BF16).astype(F32)
 
-    def pass_on(i):
-        att_copy(i).wait_recv()
-        summed = rounded(att[i, 0], wout[:, theirs]) + rounded(att[i, 1], wo[1])
-        part_s[i] = summed.astype(BF16)
-        part_copy(i).start()
-
-    def finish(i):
-        proj = rounded(att[i, 0], wout[:, own]) + rounded(att[i, 1], wo[0])
-        part_copy(i).wait_recv()
-        proj = proj + part_r[i].astype(F32)
-        lay[tok * i : tok * (i + 1), :] = (lat[i, :, own].astype(F32) + proj).astype(BF16)
+    def pass_on(n):
+        att_copy(n).wait_recv()
+        cols, block = ((to_opp, 1), (to_pair, 3))[n % 2]
+        summed = rounded(att[n, 0], wout[:, cols]) + rounded(att[n, 1], wo[block])
+        part_s[n] = summed.astype(BF16)
+        part_copy(n).start()
+
+    def finish(n):
+        u = ORDER[n]
+        proj = rounded(att[n, 0], wout[:, own]) + rounded(att[n, 1], wo[2 * (n % 2)])
+        part_copy(n).wait_recv()
+        proj = proj + part_r[n].astype(F32)
+        done = (lat[u, :, own].astype(F32) + proj).astype(BF16)
+        lay[pl.ds(pl.multiple_of(actual(u) * tok, tok), tok), :] = done
 
     n_slots = nv * cap
 
@@ -247,32 +267,38 @@
             hit = asked[:cap, k : k + 1] == lax.broadcasted_iota(I32, (cap, nl * tok), 1)
             gsel[cap * k : cap * (k + 1), :] = hit.astype(F32).astype(BF16)
 
-    for n, i in enumerate(ORDER):
+    for n, u in enumerate(ORDER):
+        with scope(f"ask{n}"):
+            ask(u)
         with scope(f"halo{n}"):
-            kv_copy((3, 0, 2, 1)[n]).wait_recv()
+            kv_copy((0, 1, 3, 2)[n]).wait_recv()
         with scope(f"att{n}"):
-            attend(i)
-        att_copy(i).start()
+            attend(n, u)
+        att_copy(n).start()
+        if n == 0:
+            with scope("prep"):
+                prepare()
         if n == 1:
-            for k in (0, 1):
+            for k in range(4):
                 wo_copy(k).wait()
         if n > 1:
             with scope(f"pass{n}"):
-                pass_on(ORDER[n - 2])
+                pass_on(n - 2)
 
     with scope("sel_mine"):
         select_mine()
     with scope("pass4"):
-        pass_on(ORDER[2])
+        pass_on(2)
     with scope("sel_asked"):
         select_asked()
     with scope("pass5"):
-        pass_on(ORDER[3])
-    for n, i in enumerate(ORDER):
+        pass_on(3)
+    for n in range(nl):
         with scope(f"finish{n}"):
-            finish(i)
-    lay_copy = pltpu.make_async_copy(lay, lay_out, out_sem.at[0])
-    lay_copy.start()
+            finish(n)
+            lay_out[pl.ds(pl.multiple_of(actual(ORDER[n]) * tok, tok), tok), :] = lay[
+                pl.ds(pl.multiple_of(actual(ORDER[n]) * tok, tok), tok), :
+            ]
 
     for lo, hi in PICK_GROUPS:
         with scope(f"pick{lo}"):
@@ -295,16 +321,12 @@
             if hi < nv:
                 acc[...] = part
             else:
-                got[...] = part.astype(BF16)
-    got_copy = pltpu.make_async_copy(got, got_out, out_sem.at[1])
-    got_copy.start()
+                got_out[...] = part.astype(BF16)
 
     for i in range(nl):
         kv_copy(i).wait_send()
         att_copy(i).wait_send()
         part_copy(i).wait_send()
-    lay_copy.wait()
-    got_copy.wait()
 
 
 def per_device(nv, latents, norm_gain, w_qkv, w_out, intersection, match_block, match_row, confidence):
@@ -312,7 +334,7 @@
     sub = w_qkv.shape[2]
     rows = nl * tok
     cap = 2 * rows // nv
-    here = pl.BlockSpec(memory_space=pl.ANY)
+    here = pl.BlockSpec(memory_space=pltpu.HBM)
     dma = pltpu.SemaphoreType.DMA
     vmem = pltpu.VMEM
     lanes = 128
@@ -320,7 +342,7 @@
         functools.partial(kernel, nv, nl * nv, cap),
         out_shape=[jax.ShapeDtypeStruct((rows, sub), BF16)] * 2,
         in_specs=[here] * 7,
-        out_specs=[here] * 2,
+        out_specs=[pl.BlockSpec(memory_space=pltpu.VMEM)] * 2,
         scratch_shapes=[
             vmem((nl, tok, width), BF16),
             vmem((1, width), F32),
@@ -332,7 +354,7 @@
             vmem((nl + 4, tok, 2 * sub), BF16),
             vmem((nl, tok, sub), BF16),
             vmem((nl, 2, tok, sub), BF16),
-            vmem((2, sub, sub), BF16),
+            vmem((4, sub, sub), BF16),
             vmem((nl, tok, sub), BF16),
             vmem((nl, tok, sub), BF16),
             vmem((rows, sub), BF16),
@@ -344,14 +366,14 @@
             vmem((nv, cap, sub), BF16),
             vmem((nv, cap, sub), BF16),
             vmem((rows, sub), F32),
-            vmem((rows, sub), BF16),
-            dma((12,)), dma((2,)),
-            dma((nl,)), dma((nl,)), dma((2,)), dma((2,)),
+            vmem((nl, tok, width), BF16),
+            dma((12,)),
+            dma((nl,)), dma((nl,)), dma((4,)), dma((4,)),
             dma((nl,)), dma((nl,)), dma((nl,)), dma((nl,)),
             dma((nv,)), dma((nv,)), dma((nv,)), dma((nv,)),
         ],
         compiler_params=pltpu.CompilerParams(
-            collective_id=0, has_side_effects=True, vmem_limit_bytes=60 * 1024 * 1024
+            collective_id=0, has_side_effects=True, vmem_limit_bytes=VMEM_MIB * 1024 * 1024
         ),
     )(
         latents,
@@ -363,7 +385,7 @@
         match_row.reshape(rows // lanes, lanes),
     )
     mine = lay.astype(F32)
-    refined = mine + COUPLING * confidence[:, None] * (got.astype(F32) - mine)
+    refined = mine + COUPLING * (confidence[:, None] * (got.astype(F32) - mine))
     return refined.reshape(nl, tok, sub)
 
 

time: 56 us -> 52.2 us (0.932)
  Pallas kernels: 52.7 us -> 49.6 us
  other arithmetic: 3.17 us -> 2.5 us
    pallas_call x1, Pallas kernels: 52.7 us -> 49.6 us  [per_device(): pl.pallas_call(functools.partial(kernel, nv, nl * nv, cap), out_shape=[ja...]
    mul x1 -> x0, other arithmetic: 0.69 us -> none  [per_device(): refined = mine + COUPLING * confidence[:, None] * (got.astype(F32) - mine)]
where the time goes in v3:
time: 52.2 us; the launch traced here: 52.1 us
  Pallas kernels  49.6 us (95%)
  other arithmetic  2.5 us (5%)
    pallas_call x1, Pallas kernels, per_device(): pl.pallas_call(functools.partial(kernel, nv, nl * nv, cap), out_shape=[ja...  49.6 us
    add x1, other arithmetic, per_device(): refined = mine + COUPLING * (confidence[:, None] * (got.astype(F32) - mine))  2.5 us

profile of v3, /device:TPU:1, one launch (start us, length us, event | category | flops | bytes accessed | tf_op | source)
XLA Modules:
  0.0 52.1 jit_solution(7044495664894908595)
XLA Ops:
  0.0 0.0 copy-start
  0.0 49.6 %shard_map.82 = (bf16[1024,256]{1,0:T(8,128)(2,1)}, bf16[1024,256]{1,0:T(8,128)(2,1)}) custom-call(bf16[4,256,1024]{2,1,0:T(8,128)(2,1)} %lat_h.1, f32[1,1024]{1,0:T(1,128)} %bitcast.5, bf16[3,1024,256]{2,1,0:T(8,128)(2,1)} %wqkv_h.1, bf16[256,1024]{1,0:T(8,128)(2,1)} %wout_h.1, s32[2,128]{1,0:T(2,128)} %bitcast.8, s32[8,128]{1,0:T(8,128)} %bitcast.6, ...), custom_call_target="tpu_custom_call" | custom-call | tf_op jit(solution)/shard_map/pallas_call | solution.py:341
  49.6 0.0 copy-done
  49.6 2.5 %convert_add_fusion = f32[1024,256]{1,0:T(8,128)} fusion(bf16[1024,256]{1,0:T(8,128)(2,1)} %get-tuple-element.7, bf16[1024,256]{1,0:T(8,128)(2,1)} %get-tuple-element.8, f32[1024]{0:T(1024)S(1)} %copy-done), kind=kLoop, calls=%fused_computation | loop fusion | flops 1572864 | bytes 2101248 | tf_op jit(solution)/shard_map/add | solution.py:388
Async XLA Ops:
  0.0 49.6 %copy-start = (f32[1024]{0:T(1024)S(1)}, f32[1024]{0:T(1024)}, u32[]{:S(2)}) copy-start(f32[1024]{0:T(1024)} %param.15) | copy-start | bytes 12292

commit v4 on v3

--- a/solution.py
+++ b/solution.py
@@ -11,6 +11,7 @@
 F32, BF16, I32 = jnp.float32, jnp.bfloat16, jnp.int32
 EPSILON = 1e-06
 COUPLING = 0.5
+LOG2_E = 1.4426950408889634
 HEAD_DIM = 64
 ORDER = (1, 0, 2, 3)
 SIDE = 4
@@ -26,7 +27,7 @@
     key=lambda p: (-ring_steps(p[0]) - ring_steps(p[1]), -p[2]),
 )
 PICK_GROUPS = ((0, 4), (4, 8), (8, 16), (16, 24), (24, 32))
-TAKE_GROUPS = ((0, 8), (8, 16), (16, 24), (24, 32))
+TAKE_GROUPS = ((0, 8), (8, 16), (16, 24), (24, 28), (28, 32))
 
 
 def dot(a, b):
@@ -35,6 +36,11 @@
 
 def dot_nt(a, b):
     return lax.dot_general(a, b, (((1,), (1,)), ((), ())), preferred_element_type=F32)
+
+
+def value_rows(h):
+    start = 256 + (2 * HEAD_DIM + 16) * (h // 2) + (h % 2) * HEAD_DIM
+    return start, start + 16 * (h % 2)
 
 
 def scope(name):
@@ -46,8 +52,8 @@
     lat_h, gain_h, wqkv_h, wout_h, inter_h, mb_h, mr_h,
     lay_out, got_out,
     lat, gain, wqkv, wout, inter, mb, mr,
-    kv, q, att, wo, part_s, part_r, lay, gsel, fsel, idxs, reqo, reqi, rows, reps, acc, normed,
-    in_sem, kv_s, kv_r, wo_s, wo_r, at_s, at_r, pt_s, pt_r, rq_s, rq_r, rp_s, rp_r,
+    kv, q, att, wo, part_s, part_r, lay, gsel, fsel, idxs, reqo, reqi, rows, reps, acc, normed, turned,
+    in_sem, kv_s, kv_r, wo_s, wo_r, ws_s, ws_r, at_s, at_r, pt_s, pt_r, rq_s, rq_r, rp_s, rp_r,
 ):
     nl, tok, width = lat.shape
     sub = wqkv.shape[2]
@@ -107,19 +113,36 @@
         target = partner if u < 2 else beyond
         return remote(kv.at[2 + u], kv.at[slot], kv_s.at[u], kv_r.at[u], (target, z))
 
+    half = sub // 2
+    my_half = pl.ds(pl.multiple_of(pc * half, half), half)
+
     def wo_copy(n):
         cols = pl.ds(pl.multiple_of((pair, far, opp, far)[n] * sub, sub), sub)
         target = (pair, opp)[n // 2]
-        return remote(wout.at[:, cols], wo.at[n], wo_s.at[n], wo_r.at[n], (me, target))
+        return remote(
+            wout.at[my_half, cols], wo.at[n, my_half], wo_s.at[n], wo_r.at[n], (me, target)
+        )
+
+    def wo_share(n):
+        block = wo.at[n, my_half]
+        return remote(block, block, ws_s.at[n], ws_r.at[n], (partner, z))
 
     def ways(n):
         return (pair, opp) if n % 2 == 0 else (opp, pair)
 
-    def att_copy(n):
-        return remote(att.at[n, 0], att.at[n, 1], at_s.at[n], at_r.at[n], (me, ways(n)[0]))
-
-    def part_copy(n):
-        return remote(part_s.at[n], part_r.at[n], pt_s.at[n], pt_r.at[n], (me, ways(n)[1]))
+    def pieces(n):
+        size = tok // 2 if n == nl - 1 else tok
+        return [(c, pl.ds(c * size, size)) for c in range(tok // size)]
+
+    def att_copy(n, c, part):
+        return remote(
+            att.at[n, 0, part], att.at[n, 1, part], at_s.at[n, c], at_r.at[n, c], (me, ways(n)[0])
+        )
+
+    def part_copy(n, c, part):
+        return remote(
+            part_s.at[n, part], part_r.at[n, part], pt_s.at[n, c], pt_r.at[n, c], (me, ways(n)[1])
+        )
 
     def req_copy(o):
         return remote(reqo.at[o], reqi.at[o], rq_s.at[o], rq_r.at[o], (away(o, 1), z))
@@ -137,10 +160,15 @@
             normed[u] = x
             if n == 0:
                 in_k.wait()
-            kv[2 + u, :, :sub] = dot(x, wqkv[1]).astype(BF16)
+            kv[2 + u, :tok, :] = dot(x, wqkv[1]).astype(BF16)
             if n == 0:
                 in_v.wait()
-            kv[2 + u, :, sub:] = dot(x, wqkv[2]).astype(BF16)
+            values = jnp.transpose(dot(x, wqkv[2])).astype(BF16)
+            for h in range(sub // HEAD_DIM):
+                top, first_row = value_rows(h)
+                kv[2 + u, first_row : first_row + HEAD_DIM, :] = values[HEAD_DIM * h : HEAD_DIM * (h + 1)]
+                if h % 2 == 0:
+                    kv[2 + u, first_row + HEAD_DIM : first_row + HEAD_DIM + 16, :] = jnp.ones((16, tok), BF16)
         if n == 2:
             with scope("greeted"):
                 pl.semaphore_wait(barrier, nv + 1)
@@ -154,9 +182,10 @@
     for copy in in_small:
         copy.wait()
 
-    def ask(u):
-        found = dot(normed[u], wqkv[0]).astype(BF16).astype(F32)
-        q[u] = (found * HEAD_DIM ** (-0.5)).astype(BF16)
+    def ask(begin, end):
+        found = dot(normed[begin:end].reshape((end - begin) * tok, width), wqkv[0])
+        found = (found * (HEAD_DIM ** (-0.5) * LOG2_E)).astype(BF16)
+        q[begin:end] = found.reshape(end - begin, tok, sub)
 
     lanes = mb.shape[1]
 
@@ -204,29 +233,35 @@
                 back = d * (1 - pc) if d > 0 else -d * pc
                 source = lax.rem(a - back + views_total, views_total)
                 present = inter[abs(d) - 1, source]
-                bias.append((present.astype(F32) - 1.0) * 1e30)
-        for t in range(sub // (2 * HEAD_DIM)):
-            k_cols = slice(2 * HEAD_DIM * t, 2 * HEAD_DIM * (t + 1))
-            v_cols = slice(sub + 2 * HEAD_DIM * t, sub + 2 * HEAD_DIM * (t + 1))
-            both = q[i, :, k_cols]
-            done = []
-            for mine in (first, jnp.logical_not(first)):
-                query = jnp.where(mine, both, jnp.zeros_like(both))
-                scores = []
-                for j in range(5):
-                    s = dot_nt(query, kv[i + j, :, k_cols])
-                    scores.append(s if bias[j] is None else s + bias[j])
-                top = functools.reduce(jnp.maximum, scores)
-                top = jnp.max(top, axis=-1, keepdims=True)
-                numer, total = None, None
-                for j in range(5):
-                    p = jnp.exp(scores[j] - top)
-                    total = p if total is None else total + p
-                    part = dot(p.astype(BF16), kv[i + j, :, v_cols])
-                    numer = part if numer is None else numer + part
-                total = jnp.sum(total, axis=-1, keepdims=True)
-                done.append(numer / total)
-            att[n, 0, :, k_cols] = jnp.where(first, done[0], done[1]).astype(BF16)
+                bias.append((1.0 - present.astype(F32)) * 1e30)
+        heads = sub // HEAD_DIM
+        scores = []
+        for h in range(heads):
+            cols = slice(2 * HEAD_DIM * (h // 2), 2 * HEAD_DIM * (h // 2 + 1))
+            both = q[i, :, cols]
+            mine = first if h % 2 == 0 else jnp.logical_not(first)
+            query = jnp.where(mine, both, jnp.zeros_like(both))
+            tiles = []
+            for j in range(5):
+                s = dot_nt(kv[i + j, :tok, cols], query)
+                high = jnp.max(s.reshape(tok // 8, 8, tok), axis=0)
+                tiles.append((s, high if bias[j] is None else high - bias[j]))
+            scores.append(tiles)
+        for h in range(heads):
+            top = functools.reduce(jnp.maximum, [high for _, high in scores[h]])
+            top = jnp.max(top, axis=0, keepdims=True)
+            found = None
+            begin, _ = value_rows(h)
+            for j in range(5):
+                p = jnp.exp2(scores[h][j][0] - (top if bias[j] is None else top + bias[j]))
+                part = dot(kv[i + j, begin : begin + HEAD_DIM + 16, :], p.astype(BF16))
+                found = part if found is None else found + part
+            if h % 2 == 0:
+                numer, total = found[:HEAD_DIM], found[HEAD_DIM : HEAD_DIM + 1]
+            else:
+                numer, total = found[16:], found[0:1]
+            turned[HEAD_DIM * h : HEAD_DIM * (h + 1), :] = numer / total
+        att[n, 0] = jnp.transpose(turned[...]).astype(BF16)
 
     own, to_pair, to_opp = (
         pl.ds(pl.multiple_of(g * sub, sub), sub) for g in (z, pair, opp)
@@ -236,16 +271,18 @@
         return dot(a, b).astype(BF16).astype(F32)
 
     def pass_on(n):
-        att_copy(n).wait_recv()
         cols, block = ((to_opp, 1), (to_pair, 3))[n % 2]
-        summed = rounded(att[n, 0], wout[:, cols]) + rounded(att[n, 1], wo[block])
-        part_s[n] = summed.astype(BF16)
-        part_copy(n).start()
+        for c, part in pieces(n):
+            att_copy(n, c, part).wait_recv()
+            summed = rounded(att[n, 0, part], wout[:, cols]) + rounded(att[n, 1, part], wo[block])
+            part_s[n, part] = summed.astype(BF16)
+            part_copy(n, c, part).start()
 
     def finish(n):
         u = ORDER[n]
         proj = rounded(att[n, 0], wout[:, own]) + rounded(att[n, 1], wo[2 * (n % 2)])
-        part_copy(n).wait_recv()
+        for c, part in pieces(n):
+            part_copy(n, c, part).wait_recv()
         proj = proj + part_r[n].astype(F32)
         done = (lat[u, :, own].astype(F32) + proj).astype(BF16)
         lay[pl.ds(pl.multiple_of(actual(u) * tok, tok), tok), :] = done
@@ -268,31 +305,36 @@
             gsel[cap * k : cap * (k + 1), :] = hit.astype(F32).astype(BF16)
 
     for n, u in enumerate(ORDER):
-        with scope(f"ask{n}"):
-            ask(u)
         with scope(f"halo{n}"):
             kv_copy((0, 1, 3, 2)[n]).wait_recv()
         with scope(f"att{n}"):
+            if n == 0:
+                ask(0, nl)
             attend(n, u)
-        att_copy(n).start()
-        if n == 0:
-            with scope("prep"):
-                prepare()
+        for c, part in pieces(n):
+            att_copy(n, c, part).start()
         if n == 1:
             for k in range(4):
                 wo_copy(k).wait()
+                wo_share(k).start()
+        if n == 2:
+            with scope("wo"):
+                for k in range(4):
+                    wo_share(k).wait()
         if n > 1:
             with scope(f"pass{n}"):
                 pass_on(n - 2)
 
+    with scope("prep"):
+        prepare()
     with scope("sel_mine"):
         select_mine()
     with scope("pass4"):
         pass_on(2)
+    with scope("pass5"):
+        pass_on(3)
     with scope("sel_asked"):
         select_asked()
-    with scope("pass5"):
-        pass_on(3)
     for n in range(nl):
         with scope(f"finish{n}"):
             finish(n)
@@ -325,8 +367,9 @@
 
     for i in range(nl):
         kv_copy(i).wait_send()
-        att_copy(i).wait_send()
-        part_copy(i).wait_send()
+        for c, part in pieces(i):
+            att_copy(i, c, part).wait_send()
+            part_copy(i, c, part).wait_send()
 
 
 def per_device(nv, latents, norm_gain, w_qkv, w_out, intersection, match_block, match_row, confidence):
@@ -351,7 +394,7 @@
             pltpu.SMEM(intersection.shape[::-1], I32),
             vmem((rows // lanes, lanes), I32),
             vmem((rows // lanes, lanes), I32),
-            vmem((nl + 4, tok, 2 * sub), BF16),
+            vmem((nl + 4, 2 * tok + 32, sub), BF16),
             vmem((nl, tok, sub), BF16),
             vmem((nl, 2, tok, sub), BF16),
             vmem((4, sub, sub), BF16),
@@ -367,9 +410,10 @@
             vmem((nv, cap, sub), BF16),
             vmem((rows, sub), F32),
             vmem((nl, tok, width), BF16),
+            vmem((sub, tok), F32),
             dma((12,)),
-            dma((nl,)), dma((nl,)), dma((4,)), dma((4,)),
-            dma((nl,)), dma((nl,)), dma((nl,)), dma((nl,)),
+            dma((nl,)), dma((nl,)), dma((4,)), dma((4,)), dma((4,)), dma((4,)),
+            dma((nl, 2)), dma((nl, 2)), dma((nl, 2)), dma((nl, 2)),
             dma((nv,)), dma((nv,)), dma((nv,)), dma((nv,)),
         ],
         compiler_params=pltpu.CompilerParams(

time: 52.2 us -> 50.5 us (0.967)
  Pallas kernels: 49.6 us -> 47.8 us
    pallas_call x1, Pallas kernels: 49.6 us -> 47.8 us  [per_device(): pl.pallas_call(functools.partial(kernel, nv, nl * nv, cap), out_shape=[ja...]
where the time goes in v4:
time: 50.5 us; the launch traced here: 50.3 us
  Pallas kernels  47.8 us (95%)
  other arithmetic  2.5 us (5%)
    pallas_call x1, Pallas kernels, per_device(): pl.pallas_call(functools.partial(kernel, nv, nl * nv, cap), out_shape=[ja...  47.8 us
    add x1, other arithmetic, per_device(): refined = mine + COUPLING * (confidence[:, None] * (got.astype(F32) - mine))  2.5 us

profile of v4, /device:TPU:1, one launch (start us, length us, event | category | flops | bytes accessed | tf_op | source)
XLA Modules:
  0.0 50.3 jit_solution(17057386053981269307)
XLA Ops:
  0.0 0.0 copy-start
  0.0 47.8 %shard_map.82 = (bf16[1024,256]{1,0:T(8,128)(2,1)}, bf16[1024,256]{1,0:T(8,128)(2,1)}) custom-call(bf16[4,256,1024]{2,1,0:T(8,128)(2,1)} %lat_h.1, f32[1,1024]{1,0:T(1,128)} %bitcast.5, bf16[3,1024,256]{2,1,0:T(8,128)(2,1)} %wqkv_h.1, bf16[256,1024]{1,0:T(8,128)(2,1)} %wout_h.1, s32[2,128]{1,0:T(2,128)} %bitcast.8, s32[8,128]{1,0:T(8,128)} %bitcast.6, ...), custom_call_target="tpu_custom_call" | custom-call | tf_op jit(solution)/shard_map/pallas_call | solution.py:384
  47.8 0.0 copy-done
  47.8 2.5 %convert_add_fusion = f32[1024,256]{1,0:T(8,128)} fusion(bf16[1024,256]{1,0:T(8,128)(2,1)} %get-tuple-element.7, bf16[1024,256]{1,0:T(8,128)(2,1)} %get-tuple-element.8, f32[1024]{0:T(1024)S(1)} %copy-done), kind=kLoop, calls=%fused_computation | loop fusion | flops 1572864 | bytes 2101248 | tf_op jit(solution)/shard_map/add | solution.py:432
Async XLA Ops:
  0.0 47.8 %copy-start = (f32[1024]{0:T(1024)S(1)}, f32[1024]{0:T(1024)}, u32[]{:S(2)}) copy-start(f32[1024]{0:T(1024)} %param.15) | copy-start | bytes 12292

commit v5 on v4

--- a/solution.py
+++ b/solution.py
@@ -52,8 +52,8 @@
     lat_h, gain_h, wqkv_h, wout_h, inter_h, mb_h, mr_h,
     lay_out, got_out,
     lat, gain, wqkv, wout, inter, mb, mr,
-    kv, q, att, wo, part_s, part_r, lay, gsel, fsel, idxs, reqo, reqi, rows, reps, acc, normed, turned,
-    in_sem, kv_s, kv_r, wo_s, wo_r, ws_s, ws_r, at_s, at_r, pt_s, pt_r, rq_s, rq_r, rp_s, rp_r,
+    kv, q, att, wo, part_s, part_r, lay, gsel, fsel, idxs, reqo, reqi, rows, reps, acc, normed, turned, got,
+    in_sem, lay_sem, got_sem, kv_s, kv_r, wo_s, wo_r, ws_s, ws_r, at_s, at_r, pt_s, pt_r, rq_s, rq_r, rp_s, rp_r,
 ):
     nl, tok, width = lat.shape
     sub = wqkv.shape[2]
@@ -128,7 +128,7 @@
         return remote(block, block, ws_s.at[n], ws_r.at[n], (partner, z))
 
     def ways(n):
-        return (pair, opp) if n % 2 == 0 else (opp, pair)
+        return (opp, pair) if n % 2 == 0 else (pair, opp)
 
     def pieces(n):
         size = tok // 2 if n == nl - 1 else tok
@@ -271,16 +271,24 @@
         return dot(a, b).astype(BF16).astype(F32)
 
     def pass_on(n):
-        cols, block = ((to_opp, 1), (to_pair, 3))[n % 2]
+        cols, block = ((to_pair, 3), (to_opp, 1))[n % 2]
         for c, part in pieces(n):
             att_copy(n, c, part).wait_recv()
             summed = rounded(att[n, 0, part], wout[:, cols]) + rounded(att[n, 1, part], wo[block])
             part_s[n, part] = summed.astype(BF16)
             part_copy(n, c, part).start()
 
+    def lay_copy(n):
+        here = pl.ds(pl.multiple_of(actual(ORDER[n]) * tok, tok), tok)
+        return pltpu.make_async_copy(lay.at[here], lay_out.at[here], lay_sem.at[n])
+
+    def got_copy(c):
+        here = pl.ds(c * tok, tok)
+        return pltpu.make_async_copy(got.at[here], got_out.at[here], got_sem.at[c])
+
     def finish(n):
         u = ORDER[n]
-        proj = rounded(att[n, 0], wout[:, own]) + rounded(att[n, 1], wo[2 * (n % 2)])
+        proj = rounded(att[n, 0], wout[:, own]) + rounded(att[n, 1], wo[2 - 2 * (n % 2)])
         for c, part in pieces(n):
             part_copy(n, c, part).wait_recv()
         proj = proj + part_r[n].astype(F32)
@@ -317,30 +325,28 @@
             for k in range(4):
                 wo_copy(k).wait()
                 wo_share(k).start()
-        if n == 2:
-            with scope("wo"):
-                for k in range(4):
-                    wo_share(k).wait()
-        if n > 1:
-            with scope(f"pass{n}"):
-                pass_on(n - 2)
-
+
+    with scope("wo"):
+        for k in range(4):
+            wo_share(k).wait()
+    with scope("pass1"):
+        pass_on(1)
+    with scope("pass0"):
+        pass_on(0)
     with scope("prep"):
         prepare()
     with scope("sel_mine"):
         select_mine()
-    with scope("pass4"):
+    with scope("pass2"):
         pass_on(2)
-    with scope("pass5"):
+    with scope("pass3"):
         pass_on(3)
     with scope("sel_asked"):
         select_asked()
     for n in range(nl):
         with scope(f"finish{n}"):
             finish(n)
-            lay_out[pl.ds(pl.multiple_of(actual(ORDER[n]) * tok, tok), tok), :] = lay[
-                pl.ds(pl.multiple_of(actual(ORDER[n]) * tok, tok), tok), :
-            ]
+            lay_copy(n).start()
 
     for lo, hi in PICK_GROUPS:
         with scope(f"pick{lo}"):
@@ -357,19 +363,59 @@
             for o in range(lo, min(hi, nv - 1)):
                 rep_copy(o).wait()
             block = reps[lo:hi].reshape((hi - lo) * cap, sub)
-            part = dot(fsel[:, cap * lo : cap * hi], block)
-            if lo > 0:
-                part = acc[...] + part
             if hi < nv:
-                acc[...] = part
+                part = dot(fsel[:, cap * lo : cap * hi], block)
+                acc[...] = part if lo == 0 else acc[...] + part
             else:
-                got_out[...] = part.astype(BF16)
-
-    for i in range(nl):
-        kv_copy(i).wait_send()
-        for c, part in pieces(i):
-            att_copy(i, c, part).wait_send()
-            part_copy(i, c, part).wait_send()
+                for c in range(nl):
+                    here = slice(c * tok, (c + 1) * tok)
+                    part = dot(fsel[here, cap * lo : cap * hi], block)
+                    got[here, :] = (acc[here, :] + part).astype(BF16)
+                    got_copy(c).start()
+
+    with scope("sent"):
+        for i in range(nl):
+            kv_copy(i).wait_send()
+            for c, part in pieces(i):
+                att_copy(i, c, part).wait_send()
+                part_copy(i, c, part).wait_send()
+    with scope("stored"):
+        for c in range(nl):
+            lay_copy(c).wait()
+            got_copy(c).wait()
+
+
+def blend(conf_h, lay_h, got_h, out_h, conf, lay, got, out, conf_sem, lay_sem, got_sem, out_sem):
+    pieces, size, _ = lay.shape
+    lanes = conf.shape[1]
+    first = pltpu.make_async_copy(conf_h, conf, conf_sem.at[0])
+    first.start()
+    loads, stores = [], []
+    for c in range(pieces):
+        here = pl.ds(c * size, size)
+        loads.append(
+            (
+                pltpu.make_async_copy(lay_h.at[here], lay.at[c], lay_sem.at[c]),
+                pltpu.make_async_copy(got_h.at[here], got.at[c], got_sem.at[c]),
+            )
+        )
+        stores.append(pltpu.make_async_copy(out.at[c], out_h.at[here], out_sem.at[c]))
+        for copy in loads[c]:
+            copy.start()
+    first.wait()
+    weight = COUPLING * jnp.transpose(conf[...])
+    for c in range(pieces):
+        for copy in loads[c]:
+            copy.wait()
+        for k in range(size // lanes):
+            here = pl.ds(k * lanes, lanes)
+            mine = lay[c, here].astype(F32)
+            column = c * (size // lanes) + k
+            other = got[c, here].astype(F32)
+            out[c, here] = mine + weight[:, column : column + 1] * (other - mine)
+        stores[c].start()
+    for copy in stores:
+        copy.wait()
 
 
 def per_device(nv, latents, norm_gain, w_qkv, w_out, intersection, match_block, match_row, confidence):
@@ -385,7 +431,7 @@
         functools.partial(kernel, nv, nl * nv, cap),
         out_shape=[jax.ShapeDtypeStruct((rows, sub), BF16)] * 2,
         in_specs=[here] * 7,
-        out_specs=[pl.BlockSpec(memory_space=pltpu.VMEM)] * 2,
+        out_specs=[here] * 2,
         scratch_shapes=[
             vmem((nl, tok, width), BF16),
             vmem((1, width), F32),
@@ -411,7 +457,8 @@
             vmem((rows, sub), F32),
             vmem((nl, tok, width), BF16),
             vmem((sub, tok), F32),
-            dma((12,)),
+            vmem((rows, sub), BF16),
+            dma((12,)), dma((nl,)), dma((nl,)),
             dma((nl,)), dma((nl,)), dma((4,)), dma((4,)), dma((4,)), dma((4,)),
             dma((nl, 2)), dma((nl, 2)), dma((nl, 2)), dma((nl, 2)),
             dma((nv,)), dma((nv,)), dma((nv,)), dma((nv,)),
@@ -428,8 +475,20 @@
         match_block.reshape(rows // lanes, lanes),
         match_row.reshape(rows // lanes, lanes),
     )
-    mine = lay.astype(F32)
-    refined = mine + COUPLING * (confidence[:, None] * (got.astype(F32) - mine))
+    pieces = 4
+    refined = pl.pallas_call(
+        blend,
+        out_shape=jax.ShapeDtypeStruct((rows, sub), F32),
+        in_specs=[here] * 3,
+        out_specs=here,
+        scratch_shapes=[
+            vmem((rows // lanes, lanes), F32),
+            vmem((pieces, rows // pieces, sub), BF16),
+            vmem((pieces, rows // pieces, sub), BF16),
+            vmem((pieces, rows // pieces, sub), F32),
+            dma((1,)), dma((pieces,)), dma((pieces,)), dma((pieces,)),
+        ],
+    )(confidence.reshape(rows // lanes, lanes), lay, got)
     return refined.reshape(nl, tok, sub)
 
 

time: 50.5 us -> 49.8 us (0.986)
  other arithmetic: 2.5 us -> 0 us
  Pallas kernels: 47.8 us -> 49.5 us
    add x1 -> x0, other arithmetic: 2.5 us -> none  [per_device(): refined = mine + COUPLING * (confidence[:, None] * (got.astype(F32) - mine))]
    pallas_call x0 -> x1, Pallas kernels: none -> 2.37 us  [per_device(): pl.pallas_call(blend, out_shape=jax.ShapeDtypeStruct((rows, sub), F32), i...]
    pallas_call x1, Pallas kernels: 47.8 us -> 47.2 us  [per_device(): pl.pallas_call(functools.partial(kernel, nv, nl * nv, cap), out_shape=[ja...]
where the time goes in v5:
time: 49.8 us; the launch traced here: 49.7 us
  Pallas kernels  49.5 us (99%)
    pallas_call x1, Pallas kernels, per_device(): pl.pallas_call(functools.partial(kernel, nv, nl * nv, cap), out_shape=[ja...  47.2 us
    pallas_call x1, Pallas kernels, per_device(): pl.pallas_call(blend, out_shape=jax.ShapeDtypeStruct((rows, sub), F32), i...  2.37 us

profile of v5, /device:TPU:1, one launch (start us, length us, event | category | flops | bytes accessed | tf_op | source)
XLA Modules:
  0.0 49.7 jit_solution(7256759276282816386)
XLA Ops:
  0.0 47.2 %shard_map.82 = (bf16[1024,256]{1,0:T(8,128)(2,1)}, bf16[1024,256]{1,0:T(8,128)(2,1)}) custom-call(bf16[4,256,1024]{2,1,0:T(8,128)(2,1)} %lat_h.1, f32[1,1024]{1,0:T(1,128)} %bitcast.7, bf16[3,1024,256]{2,1,0:T(8,128)(2,1)} %wqkv_h.1, bf16[256,1024]{1,0:T(8,128)(2,1)} %wout_h.1, s32[2,128]{1,0:T(2,128)} %bitcast.10, s32[8,128]{1,0:T(8,128)} %bitcast.8, ...), custom_call_target="tpu_custom_call" | custom-call | tf_op jit(solution)/shard_map/pallas_call | solution.py:430
  47.2 2.4 %shard_map.83 = f32[1024,256]{1,0:T(8,128)} custom-call(f32[8,128]{1,0:T(8,128)} %bitcast.6, bf16[1024,256]{1,0:T(8,128)(2,1)} %get-tuple-element.7.lay_h, bf16[1024,256]{1,0:T(8,128)(2,1)} %get-tuple-element.8.got_h), custom_call_target="tpu_custom_call" | custom-call | tf_op jit(solution)/shard_map/pallas_call | solution.py:479

commit v6 on v5

--- a/solution.py
+++ b/solution.py
@@ -27,7 +27,7 @@
     key=lambda p: (-ring_steps(p[0]) - ring_steps(p[1]), -p[2]),
 )
 PICK_GROUPS = ((0, 4), (4, 8), (8, 16), (16, 24), (24, 32))
-TAKE_GROUPS = ((0, 8), (8, 16), (16, 24), (24, 28), (28, 32))
+TAKE_GROUPS = ((0, 8), (8, 16), (16, 24), (24, 32))
 
 
 def dot(a, b):
@@ -52,7 +52,7 @@
     lat_h, gain_h, wqkv_h, wout_h, inter_h, mb_h, mr_h,
     lay_out, got_out,
     lat, gain, wqkv, wout, inter, mb, mr,
-    kv, q, att, wo, part_s, part_r, lay, gsel, fsel, idxs, reqo, reqi, rows, reps, acc, normed, turned, got,
+    kv, q, att, wo, part_s, part_r, lay, gsel, fsel, idxs, reqo, reqi, rows, reps, acc, normed, turned, got, base,
     in_sem, lay_sem, got_sem, kv_s, kv_r, wo_s, wo_r, ws_s, ws_r, at_s, at_r, pt_s, pt_r, rq_s, rq_r, rp_s, rp_r,
 ):
     nl, tok, width = lat.shape
@@ -139,53 +139,22 @@
             att.at[n, 0, part], att.at[n, 1, part], at_s.at[n, c], at_r.at[n, c], (me, ways(n)[0])
         )
 
-    def part_copy(n, c, part):
+    def part_copy(n, f, c, part):
         return remote(
-            part_s.at[n, part], part_r.at[n, part], pt_s.at[n, c], pt_r.at[n, c], (me, ways(n)[1])
+            part_s.at[f, n, part], part_r.at[f, n, part],
+            pt_s.at[n, 2 * f + c], pt_r.at[n, 2 * f + c], (me, ways(n)[1]),
         )
 
     def req_copy(o):
         return remote(reqo.at[o], reqi.at[o], rq_s.at[o], rq_r.at[o], (away(o, 1), z))
 
-    def rep_copy(o):
-        return remote(rows.at[o], reps.at[o], rp_s.at[o], rp_r.at[o], (away(o, -1), z))
-
-    in_gain.wait()
-    for n, u in enumerate((3, 2, 0, 1)):
-        with scope(f"proj{n}"):
-            in_lat[u].wait()
-            wide = lat[u].astype(F32)
-            mean_square = jnp.mean(wide * wide, axis=-1, keepdims=True)
-            x = (wide * lax.rsqrt(mean_square + EPSILON) * gain[...]).astype(BF16)
-            normed[u] = x
-            if n == 0:
-                in_k.wait()
-            kv[2 + u, :tok, :] = dot(x, wqkv[1]).astype(BF16)
-            if n == 0:
-                in_v.wait()
-            values = jnp.transpose(dot(x, wqkv[2])).astype(BF16)
-            for h in range(sub // HEAD_DIM):
-                top, first_row = value_rows(h)
-                kv[2 + u, first_row : first_row + HEAD_DIM, :] = values[HEAD_DIM * h : HEAD_DIM * (h + 1)]
-                if h % 2 == 0:
-                    kv[2 + u, first_row + HEAD_DIM : first_row + HEAD_DIM + 16, :] = jnp.ones((16, tok), BF16)
-        if n == 2:
-            with scope("greeted"):
-                pl.semaphore_wait(barrier, nv + 1)
-            for early in (0, 3, 2):
-                kv_copy(early).start()
-            in_wout.wait()
-            for k in range(4):
-                wo_copy(k).start()
-    kv_copy(1).start()
-    in_q.wait()
-    for copy in in_small:
-        copy.wait()
-
-    def ask(begin, end):
-        found = dot(normed[begin:end].reshape((end - begin) * tok, width), wqkv[0])
-        found = (found * (HEAD_DIM ** (-0.5) * LOG2_E)).astype(BF16)
-        q[begin:end] = found.reshape(end - begin, tok, sub)
+    def rep_copy(f, o):
+        return remote(
+            rows.at[f, o], reps.at[f, o], rp_s.at[f, o], rp_r.at[f, o], (away(o, -1), z)
+        )
+
+    fw = sub // 2
+    halves = (slice(0, fw), slice(fw, sub))
 
     lanes = mb.shape[1]
 
@@ -216,8 +185,44 @@
         for k in range(nv):
             reqo[k] = jnp.broadcast_to(requests[k : k + 1], reqo.shape[1:])
         reqi[nv - 1] = jnp.broadcast_to(requests[nv - 1 : nv], reqo.shape[1:])
-        for o in range(nv - 1):
-            req_copy(o).start()
+
+    in_gain.wait()
+    for n, u in enumerate((3, 2, 0, 1)):
+        with scope(f"proj{n}"):
+            in_lat[u].wait()
+            wide = lat[u].astype(F32)
+            mean_square = jnp.mean(wide * wide, axis=-1, keepdims=True)
+            x = (wide * lax.rsqrt(mean_square + EPSILON) * gain[...]).astype(BF16)
+            normed[u] = x
+            if n == 0:
+                in_k.wait()
+            kv[2 + u, :tok, :] = dot(x, wqkv[1]).astype(BF16)
+            if n == 0:
+                in_v.wait()
+            values = jnp.transpose(dot(x, wqkv[2])).astype(BF16)
+            for h in range(sub // HEAD_DIM):
+                top, first_row = value_rows(h)
+                kv[2 + u, first_row : first_row + HEAD_DIM, :] = values[HEAD_DIM * h : HEAD_DIM * (h + 1)]
+                if h % 2 == 0:
+                    kv[2 + u, first_row + HEAD_DIM : first_row + HEAD_DIM + 16, :] = jnp.ones((16, tok), BF16)
+        if n == 2:
+            with scope("prep"):
+                for copy in in_small:
+                    copy.wait()
+                prepare()
+            with scope("greeted"):
+                pl.semaphore_wait(barrier, nv + 1)
+            for early in (0, 3, 2):
+                kv_copy(early).start()
+            in_wout.wait()
+            for k in range(4):
+                wo_copy(k).start()
+    kv_copy(1).start()
+    in_q.wait()
+    def ask(begin, end):
+        found = dot(normed[begin:end].reshape((end - begin) * tok, width), wqkv[0])
+        found = (found * (HEAD_DIM ** (-0.5) * LOG2_E)).astype(BF16)
+        q[begin:end] = found.reshape(end - begin, tok, sub)
 
     lane = lax.broadcasted_iota(I32, (1, 2 * HEAD_DIM), 1)
     first = lane < HEAD_DIM
@@ -275,25 +280,35 @@
         for c, part in pieces(n):
             att_copy(n, c, part).wait_recv()
             summed = rounded(att[n, 0, part], wout[:, cols]) + rounded(att[n, 1, part], wo[block])
-            part_s[n, part] = summed.astype(BF16)
-            part_copy(n, c, part).start()
-
-    def lay_copy(n):
+            for f in (0, 1):
+                part_s[f, n, part] = summed[:, halves[f]].astype(BF16)
+            part_copy(n, 0, c, part).start()
+            if n == 1:
+                part_copy(n, 1, c, part).start()
+
+    def lay_copy(n, f):
         here = pl.ds(pl.multiple_of(actual(ORDER[n]) * tok, tok), tok)
-        return pltpu.make_async_copy(lay.at[here], lay_out.at[here], lay_sem.at[n])
+        return pltpu.make_async_copy(
+            lay.at[f, here], lay_out.at[here, halves[f]], lay_sem.at[n, f]
+        )
 
     def got_copy(c):
         here = pl.ds(c * tok, tok)
         return pltpu.make_async_copy(got.at[here], got_out.at[here], got_sem.at[c])
 
-    def finish(n):
+    def begin(n):
+        proj = rounded(att[n, 0], wout[:, own]) + rounded(att[n, 1], wo[2 - 2 * (n % 2)])
+        base[n] = proj
+
+    def finish(n, f):
         u = ORDER[n]
-        proj = rounded(att[n, 0], wout[:, own]) + rounded(att[n, 1], wo[2 - 2 * (n % 2)])
+        mine = pl.ds(pl.multiple_of(z * sub + f * fw, fw), fw)
         for c, part in pieces(n):
-            part_copy(n, c, part).wait_recv()
-        proj = proj + part_r[n].astype(F32)
-        done = (lat[u, :, own].astype(F32) + proj).astype(BF16)
-        lay[pl.ds(pl.multiple_of(actual(u) * tok, tok), tok), :] = done
+            part_copy(n, f, c, part).wait_recv()
+        proj = base[n, :, halves[f]] + part_r[f, n].astype(F32)
+        done = (lat[u, :, mine].astype(F32) + proj).astype(BF16)
+        lay[f, pl.ds(pl.multiple_of(actual(u) * tok, tok), tok), :] = done
+        lay_copy(n, f).start()
 
     n_slots = nv * cap
 
@@ -322,6 +337,8 @@
         for c, part in pieces(n):
             att_copy(n, c, part).start()
         if n == 1:
+            for o in range(nv - 1):
+                req_copy(o).start()
             for k in range(4):
                 wo_copy(k).wait()
                 wo_share(k).start()
@@ -333,55 +350,63 @@
         pass_on(1)
     with scope("pass0"):
         pass_on(0)
-    with scope("prep"):
-        prepare()
-    with scope("sel_mine"):
-        select_mine()
+    with scope("sel_asked"):
+        select_asked()
     with scope("pass2"):
         pass_on(2)
     with scope("pass3"):
         pass_on(3)
-    with scope("sel_asked"):
-        select_asked()
-    for n in range(nl):
-        with scope(f"finish{n}"):
-            finish(n)
-            lay_copy(n).start()
-
-    for lo, hi in PICK_GROUPS:
-        with scope(f"pick{lo}"):
-            picked = dot(gsel[cap * lo : cap * hi, :], lay[...]).astype(BF16)
-            picked = picked.reshape(hi - lo, cap, sub)
-            rows[lo:hi] = picked
-            if hi == nv:
-                reps[nv - 1] = picked[-1]
-            for o in range(lo, min(hi, nv - 1)):
-                rep_copy(o).start()
-
-    for lo, hi in TAKE_GROUPS:
-        with scope(f"take{lo}"):
-            for o in range(lo, min(hi, nv - 1)):
-                rep_copy(o).wait()
-            block = reps[lo:hi].reshape((hi - lo) * cap, sub)
-            if hi < nv:
-                part = dot(fsel[:, cap * lo : cap * hi], block)
-                acc[...] = part if lo == 0 else acc[...] + part
-            else:
-                for c in range(nl):
-                    here = slice(c * tok, (c + 1) * tok)
-                    part = dot(fsel[here, cap * lo : cap * hi], block)
-                    got[here, :] = (acc[here, :] + part).astype(BF16)
-                    got_copy(c).start()
+    for n in (0, 2, 3):
+        for c, part in pieces(n):
+            part_copy(n, 1, c, part).start()
+    with scope("sel_mine"):
+        select_mine()
+    with scope("begin"):
+        for n in range(nl):
+            begin(n)
+
+    for f in (0, 1):
+        for n in range(nl):
+            with scope(f"finish{f}{n}"):
+                finish(n, f)
+        for lo, hi in PICK_GROUPS:
+            with scope(f"pick{f}{lo}"):
+                picked = dot(gsel[cap * lo : cap * hi, :], lay[f]).astype(BF16)
+                picked = picked.reshape(hi - lo, cap, fw)
+                rows[f, lo:hi] = picked
+                if hi == nv:
+                    reps[f, nv - 1] = picked[-1]
+                for o in range(lo, min(hi, nv - 1)):
+                    rep_copy(f, o).start()
+
+    for f in (0, 1):
+        for lo, hi in TAKE_GROUPS:
+            with scope(f"take{f}{lo}"):
+                for o in range(lo, min(hi, nv - 1)):
+                    rep_copy(f, o).wait()
+                block = reps[f, lo:hi].reshape((hi - lo) * cap, fw)
+                if hi < nv:
+                    part = dot(fsel[:, cap * lo : cap * hi], block)
+                    acc[...] = part if lo == 0 else acc[...] + part
+                else:
+                    for c in range(nl):
+                        here = slice(c * tok, (c + 1) * tok)
+                        part = dot(fsel[here, cap * lo : cap * hi], block)
+                        got[here, halves[f]] = (acc[here, :] + part).astype(BF16)
+                        if f == 1:
+                            got_copy(c).start()
 
     with scope("sent"):
         for i in range(nl):
             kv_copy(i).wait_send()
             for c, part in pieces(i):
                 att_copy(i, c, part).wait_send()
-                part_copy(i, c, part).wait_send()
+                for f in (0, 1):
+                    part_copy(i, f, c, part).wait_send()
     with scope("stored"):
         for c in range(nl):
-            lay_copy(c).wait()
+            for f in (0, 1):
+                lay_copy(c, f).wait()
             got_copy(c).wait()
 
 
@@ -444,24 +469,25 @@
             vmem((nl, tok, sub), BF16),
             vmem((nl, 2, tok, sub), BF16),
             vmem((4, sub, sub), BF16),
-            vmem((nl, tok, sub), BF16),
-            vmem((nl, tok, sub), BF16),
-            vmem((rows, sub), BF16),
+            vmem((2, nl, tok, sub // 2), BF16),
+            vmem((2, nl, tok, sub // 2), BF16),
+            vmem((2, rows, sub // 2), BF16),
             vmem((nv * cap, rows), BF16),
             vmem((rows, nv * cap), BF16),
             vmem((rows // lanes, lanes), F32),
             vmem((nv, 8, lanes), I32),
             vmem((nv, 8, lanes), I32),
-            vmem((nv, cap, sub), BF16),
-            vmem((nv, cap, sub), BF16),
-            vmem((rows, sub), F32),
+            vmem((2, nv, cap, sub // 2), BF16),
+            vmem((2, nv, cap, sub // 2), BF16),
+            vmem((rows, sub // 2), F32),
             vmem((nl, tok, width), BF16),
             vmem((sub, tok), F32),
             vmem((rows, sub), BF16),
-            dma((12,)), dma((nl,)), dma((nl,)),
+            vmem((nl, tok, sub), F32),
+            dma((12,)), dma((nl, 2)), dma((nl,)),
             dma((nl,)), dma((nl,)), dma((4,)), dma((4,)), dma((4,)), dma((4,)),
-            dma((nl, 2)), dma((nl, 2)), dma((nl, 2)), dma((nl, 2)),
-            dma((nv,)), dma((nv,)), dma((nv,)), dma((nv,)),
+            dma((nl, 2)), dma((nl, 2)), dma((nl, 4)), dma((nl, 4)),
+            dma((nv,)), dma((nv,)), dma((2, nv)), dma((2, nv)),
         ],
         compiler_params=pltpu.CompilerParams(
             collective_id=0, has_side_effects=True, vmem_limit_bytes=VMEM_MIB * 1024 * 1024

time: 49.8 us -> 49.4 us (level)
  no operation moved by 1% of the time
where the time goes in v6:
time: 49.4 us; the launch traced here: 49.3 us
  Pallas kernels  49.1 us (99%)
    pallas_call x1, Pallas kernels, per_device(): pl.pallas_call(functools.partial(kernel, nv, nl * nv, cap), out_shape=[ja...  46.7 us
    pallas_call x1, Pallas kernels, per_device(): pl.pallas_call(blend, out_shape=jax.ShapeDtypeStruct((rows, sub), F32), i...  2.37 us

profile of v6, /device:TPU:1, one launch (start us, length us, event | category | flops | bytes accessed | tf_op | source)
XLA Modules:
  0.0 49.3 jit_solution(8899527156233050497)
XLA Ops:
  0.0 46.7 %shard_map.82 = (bf16[1024,256]{1,0:T(8,128)(2,1)}, bf16[1024,256]{1,0:T(8,128)(2,1)}) custom-call(bf16[4,256,1024]{2,1,0:T(8,128)(2,1)} %lat_h.1, f32[1,1024]{1,0:T(1,128)} %bitcast.7, bf16[3,1024,256]{2,1,0:T(8,128)(2,1)} %wqkv_h.1, bf16[256,1024]{1,0:T(8,128)(2,1)} %wout_h.1, s32[2,128]{1,0:T(2,128)} %bitcast.10, s32[8,128]{1,0:T(8,128)} %bitcast.8, ...), custom_call_target="tpu_custom_call" | custom-call | tf_op jit(solution)/shard_map/pallas_call | solution.py:455
  46.7 2.4 %shard_map.83 = f32[1024,256]{1,0:T(8,128)} custom-call(f32[8,128]{1,0:T(8,128)} %bitcast.6, bf16[1024,256]{1,0:T(8,128)(2,1)} %get-tuple-element.7.lay_h, bf16[1024,256]{1,0:T(8,128)(2,1)} %get-tuple-element.8.got_h), custom_call_target="tpu_custom_call" | custom-call | tf_op jit(solution)/shard_map/pallas_call | solution.py:505

commit v7 on v6

--- a/solution.py
+++ b/solution.py
@@ -27,6 +27,7 @@
     key=lambda p: (-ring_steps(p[0]) - ring_steps(p[1]), -p[2]),
 )
 PICK_GROUPS = ((0, 4), (4, 8), (8, 16), (16, 24), (24, 32))
+GROUP = 8
 TAKE_GROUPS = ((0, 8), (8, 16), (16, 24), (24, 32))
 
 
@@ -136,21 +137,32 @@
 
     def att_copy(n, c, part):
         return remote(
-            att.at[n, 0, part], att.at[n, 1, part], at_s.at[n, c], at_r.at[n, c], (me, ways(n)[0])
+            att.at[n, 0, part], att.at[n, 1, part], at_s.at[n + c], at_r.at[n + c], (me, ways(n)[0])
         )
 
     def part_copy(n, f, c, part):
         return remote(
             part_s.at[f, n, part], part_r.at[f, n, part],
-            pt_s.at[n, 2 * f + c], pt_r.at[n, 2 * f + c], (me, ways(n)[1]),
+            pt_s.at[f, n + c], pt_r.at[f, n + c], (me, ways(n)[1]),
         )
 
     def req_copy(o):
-        return remote(reqo.at[o], reqi.at[o], rq_s.at[o], rq_r.at[o], (away(o, 1), z))
+        return remote(reqo.at[o], reqi.at[o], rq_s.at[0], rq_r.at[0], (away(o, 1), z))
+
+    def all_requests():
+        here = pl.ds(0, nv - 1)
+        return remote(reqo.at[here], reqi.at[here], rq_s.at[0], rq_r.at[0], (beyond, z))
 
     def rep_copy(f, o):
+        g = o // GROUP
         return remote(
-            rows.at[f, o], reps.at[f, o], rp_s.at[f, o], rp_r.at[f, o], (away(o, -1), z)
+            rows.at[f, o], reps.at[f, o], rp_s.at[f, g], rp_r.at[f, g], (away(o, -1), z)
+        )
+
+    def reply_group(f, g):
+        here = pl.ds(g * GROUP, min(GROUP, nv - 1 - g * GROUP))
+        return remote(
+            rows.at[f, here], reps.at[f, here], rp_s.at[f, g], rp_r.at[f, g], (beyond, z)
         )
 
     fw = sub // 2
@@ -289,12 +301,12 @@
     def lay_copy(n, f):
         here = pl.ds(pl.multiple_of(actual(ORDER[n]) * tok, tok), tok)
         return pltpu.make_async_copy(
-            lay.at[f, here], lay_out.at[here, halves[f]], lay_sem.at[n, f]
+            lay.at[f, here], lay_out.at[here, halves[f]], lay_sem.at[0]
         )
 
     def got_copy(c):
         here = pl.ds(c * tok, tok)
-        return pltpu.make_async_copy(got.at[here], got_out.at[here], got_sem.at[c])
+        return pltpu.make_async_copy(got.at[here], got_out.at[here], got_sem.at[0])
 
     def begin(n):
         proj = rounded(att[n, 0], wout[:, own]) + rounded(att[n, 1], wo[2 - 2 * (n % 2)])
@@ -320,8 +332,7 @@
             fsel[lanes * c : lanes * (c + 1), :] = hit.astype(F32).astype(BF16)
 
     def select_asked():
-        for o in range(nv - 1):
-            req_copy(o).wait()
+        all_requests().wait()
         asked = jnp.transpose(reqi[:, 0, :])
         for k in range(nv):
             hit = asked[:cap, k : k + 1] == lax.broadcasted_iota(I32, (cap, nl * tok), 1)
@@ -382,8 +393,7 @@
     for f in (0, 1):
         for lo, hi in TAKE_GROUPS:
             with scope(f"take{f}{lo}"):
-                for o in range(lo, min(hi, nv - 1)):
-                    rep_copy(f, o).wait()
+                reply_group(f, lo // GROUP).wait()
                 block = reps[f, lo:hi].reshape((hi - lo) * cap, fw)
                 if hi < nv:
                     part = dot(fsel[:, cap * lo : cap * hi], block)
@@ -404,10 +414,8 @@
                 for f in (0, 1):
                     part_copy(i, f, c, part).wait_send()
     with scope("stored"):
-        for c in range(nl):
-            for f in (0, 1):
-                lay_copy(c, f).wait()
-            got_copy(c).wait()
+        pltpu.make_async_copy(got, lay_out, lay_sem.at[0]).wait()
+        pltpu.make_async_copy(got, got_out, got_sem.at[0]).wait()
 
 
 def blend(conf_h, lay_h, got_h, out_h, conf, lay, got, out, conf_sem, lay_sem, got_sem, out_sem):
@@ -484,10 +492,10 @@
             vmem((sub, tok), F32),
             vmem((rows, sub), BF16),
             vmem((nl, tok, sub), F32),
-            dma((12,)), dma((nl, 2)), dma((nl,)),
+            dma((12,)), dma((1,)), dma((1,)),
             dma((nl,)), dma((nl,)), dma((4,)), dma((4,)), dma((4,)), dma((4,)),
-            dma((nl, 2)), dma((nl, 2)), dma((nl, 4)), dma((nl, 4)),
-            dma((nv,)), dma((nv,)), dma((2, nv)), dma((2, nv)),
+            dma((nl + 1,)), dma((nl + 1,)), dma((2, nl + 1)), dma((2, nl + 1)),
+            dma((1,)), dma((1,)), dma((2, nv // GROUP)), dma((2, nv // GROUP)),
         ],
         compiler_params=pltpu.CompilerParams(
             collective_id=0, has_side_effects=True, vmem_limit_bytes=VMEM_MIB * 1024 * 1024

time: 49.4 us -> 47.5 us (0.962)
  Pallas kernels: 49.1 us -> 47.2 us
    pallas_call x1, Pallas kernels: 46.7 us -> 44.9 us  [per_device(): pl.pallas_call(functools.partial(kernel, nv, nl * nv, cap), out_shape=[ja...]
where the time goes in v7:
time: 47.5 us; the launch traced here: 47.4 us
  Pallas kernels  47.2 us (99%)
    pallas_call x1, Pallas kernels, per_device(): pl.pallas_call(functools.partial(kernel, nv, nl * nv, cap), out_shape=[ja...  44.9 us
    pallas_call x1, Pallas kernels, per_device(): pl.pallas_call(blend, out_shape=jax.ShapeDtypeStruct((rows, sub), F32), i...  2.37 us

profile of v7, /device:TPU:1, one launch (start us, length us, event | category | flops | bytes accessed | tf_op | source)
XLA Modules:
  0.0 47.4 jit_solution(1531522305464738806)
XLA Ops:
  0.0 44.9 %shard_map.82 = (bf16[1024,256]{1,0:T(8,128)(2,1)}, bf16[1024,256]{1,0:T(8,128)(2,1)}) custom-call(bf16[4,256,1024]{2,1,0:T(8,128)(2,1)} %lat_h.1, f32[1,1024]{1,0:T(1,128)} %bitcast.7, bf16[3,1024,256]{2,1,0:T(8,128)(2,1)} %wqkv_h.1, bf16[256,1024]{1,0:T(8,128)(2,1)} %wout_h.1, s32[2,128]{1,0:T(2,128)} %bitcast.10, s32[8,128]{1,0:T(8,128)} %bitcast.8, ...), custom_call_target="tpu_custom_call" | custom-call | tf_op jit(solution)/shard_map/pallas_call | solution.py:463
  44.9 2.4 %shard_map.83 = f32[1024,256]{1,0:T(8,128)} custom-call(f32[8,128]{1,0:T(8,128)} %bitcast.6, bf16[1024,256]{1,0:T(8,128)(2,1)} %get-tuple-element.7.lay_h, bf16[1024,256]{1,0:T(8,128)(2,1)} %get-tuple-element.8.got_h), custom_call_target="tpu_custom_call" | custom-call | tf_op jit(solution)/shard_map/pallas_call | solution.py:513

commit v8 on v7

--- a/solution.py
+++ b/solution.py
@@ -112,7 +112,7 @@
     def kv_copy(u):
         slot = (1, 0, nl + 3, nl + 2)[u]
         target = partner if u < 2 else beyond
-        return remote(kv.at[2 + u], kv.at[slot], kv_s.at[u], kv_r.at[u], (target, z))
+        return remote(kv.at[2 + u], kv.at[slot], kv_s.at[0], kv_r.at[u], (target, z))
 
     half = sub // 2
     my_half = pl.ds(pl.multiple_of(pc * half, half), half)
@@ -121,12 +121,12 @@
         cols = pl.ds(pl.multiple_of((pair, far, opp, far)[n] * sub, sub), sub)
         target = (pair, opp)[n // 2]
         return remote(
-            wout.at[my_half, cols], wo.at[n, my_half], wo_s.at[n], wo_r.at[n], (me, target)
+            wout.at[my_half, cols], wo.at[n, my_half], wo_s.at[0], wo_r.at[0], (me, target)
         )
 
     def wo_share(n):
         block = wo.at[n, my_half]
-        return remote(block, block, ws_s.at[n], ws_r.at[n], (partner, z))
+        return remote(block, block, ws_s.at[0], ws_r.at[0], (partner, z))
 
     def ways(n):
         return (opp, pair) if n % 2 == 0 else (pair, opp)
@@ -137,13 +137,13 @@
 
     def att_copy(n, c, part):
         return remote(
-            att.at[n, 0, part], att.at[n, 1, part], at_s.at[n + c], at_r.at[n + c], (me, ways(n)[0])
+            att.at[n, 0, part], att.at[n, 1, part], at_s.at[0], at_r.at[n + c], (me, ways(n)[0])
         )
 
     def part_copy(n, f, c, part):
         return remote(
             part_s.at[f, n, part], part_r.at[f, n, part],
-            pt_s.at[f, n + c], pt_r.at[f, n + c], (me, ways(n)[1]),
+            pt_s.at[0], pt_r.at[f, n + c], (me, ways(n)[1]),
         )
 
     def req_copy(o):
@@ -350,13 +350,14 @@
         if n == 1:
             for o in range(nv - 1):
                 req_copy(o).start()
+            blocks = wo.at[:, my_half]
+            remote(blocks, blocks, wo_s.at[0], wo_r.at[0], (me, pair)).wait()
             for k in range(4):
-                wo_copy(k).wait()
                 wo_share(k).start()
 
     with scope("wo"):
-        for k in range(4):
-            wo_share(k).wait()
+        blocks = wo.at[:, my_half]
+        remote(blocks, blocks, ws_s.at[0], ws_r.at[0], (partner, z)).wait()
     with scope("pass1"):
         pass_on(1)
     with scope("pass0"):
@@ -407,12 +408,10 @@
                             got_copy(c).start()
 
     with scope("sent"):
-        for i in range(nl):
-            kv_copy(i).wait_send()
-            for c, part in pieces(i):
-                att_copy(i, c, part).wait_send()
-                for f in (0, 1):
-                    part_copy(i, f, c, part).wait_send()
+        here = pl.ds(2, nl)
+        remote(kv.at[here], kv.at[here], kv_s.at[0], kv_r.at[0], (partner, z)).wait_send()
+        remote(att.at[:, 0], att.at[:, 0], at_s.at[0], at_r.at[0], (me, pair)).wait_send()
+        remote(part_s, part_s, pt_s.at[0], pt_r.at[0, 0], (me, pair)).wait_send()
     with scope("stored"):
         pltpu.make_async_copy(got, lay_out, lay_sem.at[0]).wait()
         pltpu.make_async_copy(got, got_out, got_sem.at[0]).wait()
@@ -493,8 +492,8 @@
             vmem((rows, sub), BF16),
             vmem((nl, tok, sub), F32),
             dma((12,)), dma((1,)), dma((1,)),
-            dma((nl,)), dma((nl,)), dma((4,)), dma((4,)), dma((4,)), dma((4,)),
-            dma((nl + 1,)), dma((nl + 1,)), dma((2, nl + 1)), dma((2, nl + 1)),
+            dma((1,)), dma((nl,)), dma((1,)), dma((1,)), dma((1,)), dma((1,)),
+            dma((1,)), dma((nl + 1,)), dma((1,)), dma((2, nl + 1)),
             dma((1,)), dma((1,)), dma((2, nv // GROUP)), dma((2, nv // GROUP)),
         ],
         compiler_params=pltpu.CompilerParams(

time: 47.5 us -> 47.3 us (level)
  no operation moved by 1% of the time
where the time goes in v8:
time: 47.3 us; the launch traced here: 47.2 us
  Pallas kernels  47 us (99%)
    pallas_call x1, Pallas kernels, per_device(): pl.pallas_call(functools.partial(kernel, nv, nl * nv, cap), out_shape=[ja...  44.6 us
    pallas_call x1, Pallas kernels, per_device(): pl.pallas_call(blend, out_shape=jax.ShapeDtypeStruct((rows, sub), F32), i...  2.37 us

profile of v8, /device:TPU:1, one launch (start us, length us, event | category | flops | bytes accessed | tf_op | source)
XLA Modules:
  0.0 47.2 jit_solution(11390287886297070441)
XLA Ops:
  0.0 44.6 %shard_map.82 = (bf16[1024,256]{1,0:T(8,128)(2,1)}, bf16[1024,256]{1,0:T(8,128)(2,1)}) custom-call(bf16[4,256,1024]{2,1,0:T(8,128)(2,1)} %lat_h.1, f32[1,1024]{1,0:T(1,128)} %bitcast.7, bf16[3,1024,256]{2,1,0:T(8,128)(2,1)} %wqkv_h.1, bf16[256,1024]{1,0:T(8,128)(2,1)} %wout_h.1, s32[2,128]{1,0:T(2,128)} %bitcast.10, s32[8,128]{1,0:T(8,128)} %bitcast.8, ...), custom_call_target="tpu_custom_call" | custom-call | tf_op jit(solution)/shard_map/pallas_call | solution.py:462
  44.6 2.4 %shard_map.83 = f32[1024,256]{1,0:T(8,128)} custom-call(f32[8,128]{1,0:T(8,128)} %bitcast.6, bf16[1024,256]{1,0:T(8,128)(2,1)} %get-tuple-element.7.lay_h, bf16[1024,256]{1,0:T(8,128)(2,1)} %get-tuple-element.8.got_h), custom_call_target="tpu_custom_call" | custom-call | tf_op jit(solution)/shard_map/pallas_call | solution.py:512
